TPU v7x, 512 devices: a 8x2x16 block of a 8x8x16 slice. The times are simulated.
512 devices in a mesh: member: 2 (over y), tile: 128 (over x, z), sub: 2 (over core).
Axes of the slice: x: 8, y: 2, z: 16, core: 2. Of those that a mesh axis runs over, the one named last changes fastest.
The devices are a block of a 8x8x16 slice.
Arguments:
- atm_state: bfloat16 [8, 524288], P(None, ('member', 'tile')), parts along dimension 1, may hold values from -6 to 6
- ocn_state: bfloat16 [4, 524288], P(None, ('member', 'tile', 'sub')), parts along dimension 1, may hold values from -6 to 6
- need_atm: int32 [2048], P(('tile', 'sub')), may hold values from 0 to 2047, as said below
- xb_need: int32 [2048], P(('tile', 'sub')), may hold values from 0 to 15
- xb_ocn: int32 [2048], P(('tile', 'sub')), may hold values from 0 to 15
- xb_count: int32 [256], P(('tile', 'sub')), may hold values from 1 to 8, as said below
- sea_mask: int32 [262144], P(('tile', 'sub')), may hold values 0 or 1
- cell_area: float32 [262144], P(('tile', 'sub')), may hold values from 0.5 to 2
- w_atm: bfloat16 [2048, 128, 128], P(('tile', 'sub')), may hold values from 0.0099487305 to 1
- w_ocn: bfloat16 [2048, 128, 128], P(('tile', 'sub')), may hold values from 0.0099487305 to 1
Outputs:
- atm_flux: float32 [4, 524288], P(None, ('member', 'tile')), parts along dimension 1
- ocn_flux: float32 [4, 524288], P(None, ('member', 'tile', 'sub')), parts along dimension 1
There are 2 independent parts, one for each index of `member`. A program takes and returns all parts, laid end to end along the dimension named above; an argument that names none is the same for every part. Nothing has to cross between parts.
Inputs may be any that keep to these rules, and one draw needn't show every extreme that they name: `need_atm`: an atmosphere block n lies on tile n // 16. A tile's list is the entries of its devices in device order; for tile t its entries 2 i and 2 i + 1 lie on tile (t + i - 8 // 2 + 1) mod 128 for i < 7, and on tile (t + 64) mod 128 for i = 7; all entries of one tile's list are distinct. `xb_need`: index into the list of the block's tile. `xb_ocn`: index among the ocean blocks of the block's tile, in device order. `xb_count`: some device has all 8 blocks live.
All inputs are finite; a program needn't handle non-finite values. No bound on the sum of `sea_mask` on one device may be relied on, other than what follows from the above.
Results may differ from a plain program's by a relative error of at most 0.0003.
Values may be sent and summed in bfloat16 or wider, within the bound.
A program may use at most 64 MiB of HBM per device.

v0:
```python
import jax
import jax.numpy as jnp
from jax import lax
from jax.sharding import PartitionSpec as P


def passed_along(block, axis, distance):
    devices = range(lax.axis_size(axis))
    route = [((i - distance) % len(devices), i) for i in devices]
    return lax.ppermute(block, axis, route)


def total_of_pieces(array, axis):
    return lax.all_gather(array, axis).sum(0)


def in_blocks(array, dim, length):
    shape = array.shape
    blocks = array.reshape(*shape[:dim], length, shape[dim] // length, *shape[dim + 1 :])
    return jnp.moveaxis(blocks, dim, 0)


def summed_on_arrival(array, axis, dim):
    length = lax.axis_size(axis)
    blocks = lax.all_to_all(in_blocks(array, dim, length), axis, 0, 0, tiled=True)
    return jnp.sum(blocks, axis=0)


def bulk_fluxes(upper_domain_vector, marine_regrid_transfer):
    (
        lowest_level_warmth,
        vapour_mixing_ratio,
        eastward_wind,
        northward_wind,
        ground_level_pressure,
        solar_radiation,
        infrared_radiation,
        rainfall_rate,
    ) = [upper_domain_vector[:, grid_box_number] for grid_box_number in range(8)]
    skin_warmth_kelvin, eastward_current, northward_current, marine_climate_coupler = [
        marine_regrid_transfer[:, grid_box_number] for grid_box_number in range(4)
    ]
    du = eastward_wind - eastward_current
    dv = northward_wind - northward_current
    speed = jnp.sqrt(du * du + dv * dv + 1.0)
    momentum_transfer_factor = (0.3 + 0.1 * jnp.tanh(ground_level_pressure)) * speed
    conductive_energy_loss = momentum_transfer_factor * (skin_warmth_kelvin - lowest_level_warmth)
    evaporative_energy_loss = momentum_transfer_factor * (
        0.5 * skin_warmth_kelvin - vapour_mixing_ratio
    )
    taux = momentum_transfer_factor * du
    tauy = momentum_transfer_factor * dv
    reflected_fraction = 0.06 + 0.1 * jax.nn.sigmoid(marine_climate_coupler)
    thermal_energy_transfer = (
        (1.0 - reflected_fraction) * solar_radiation
        + infrared_radiation
        - 0.2 * skin_warmth_kelvin
        - conductive_energy_loss
        - evaporative_energy_loss
    )
    fresh = rainfall_rate - 0.5 * evaporative_energy_loss
    return (
        jnp.stack([conductive_energy_loss, evaporative_energy_loss, taux, tauy], 1),
        jnp.stack([thermal_energy_transfer, taux, tauy, fresh], 1),
    )


def owner_offset(index, npairs, ntile):
    if index < npairs - 1:
        return index - npairs // 2 + 1
    return ntile // 2


def per_device(
    atm_state, ocn_state, need_atm, xb_need, xb_ocn, xb_count, sea_mask, cell_area, w_atm, w_ocn
):
    highest = lax.Precision.HIGHEST
    ntile = lax.axis_size("tile")
    fields_a = atm_state.shape[0]
    fields_o = ocn_state.shape[0]
    blk = w_atm.shape[1]
    nblocks = w_atm.shape[0]
    owned_blocks = atm_state.shape[1] // blk
    table = jnp.transpose(atm_state.reshape(fields_a, owned_blocks, blk), (1, 0, 2))
    wanted = lax.all_gather(need_atm, "sub", axis=0, tiled=True)
    npairs = wanted.shape[0] // 2
    pairs = (wanted % owned_blocks).reshape(npairs, 2)
    pieces = []
    asked_list = []
    for index in range(npairs):
        offset = owner_offset(index, npairs, ntile)
        asked = passed_along(pairs[index], "tile", offset)
        reply = passed_along(table[asked], "tile", -offset)
        pieces.append(reply)
        asked_list.append(asked)
    fetched = jnp.concatenate(pieces, 0)
    ocean_all = lax.all_gather(ocn_state, "sub", axis=1, tiled=True)
    ocean_table = jnp.transpose(ocean_all.reshape(fields_o, -1, blk), (1, 0, 2))
    upper_domain_vector = jnp.einsum(
        "bfj,bxj->bfx", fetched[xb_need], w_atm, preferred_element_type=jnp.float32
    )
    upper_domain_vector = (
        upper_domain_vector / jnp.sum(w_atm, axis=2, dtype=jnp.float32)[:, None, :]
    )
    marine_regrid_transfer = jnp.einsum(
        "bfj,bxj->bfx", ocean_table[xb_ocn], w_ocn, preferred_element_type=jnp.float32
    )
    marine_regrid_transfer = (
        marine_regrid_transfer / jnp.sum(w_ocn, axis=2, dtype=jnp.float32)[:, None, :]
    )
    to_atm, to_ocn = bulk_fluxes(upper_domain_vector, marine_regrid_transfer)
    live = (jnp.arange(nblocks, dtype=jnp.int32) < xb_count[0]).astype(jnp.float32)[:, None]
    weighted = cell_area.reshape(nblocks, blk) * live
    wet = weighted * sea_mask.reshape(nblocks, blk).astype(jnp.float32)
    atm_terms = jnp.concatenate([to_atm * wet[:, None, :], weighted[:, None, :]], 1)
    ocn_terms = jnp.concatenate([to_ocn * wet[:, None, :], wet[:, None, :]], 1)
    atm_cells = jnp.einsum(
        "bgx,bxj->bgj", atm_terms, w_atm, precision=highest, preferred_element_type=jnp.float32
    )
    ocn_cells = jnp.einsum(
        "bgx,bxj->bgj", ocn_terms, w_ocn, precision=highest, preferred_element_type=jnp.float32
    )
    list_len = fetched.shape[0]
    select_a = (xb_need[:, None] == jnp.arange(list_len, dtype=jnp.int32)[None, :]).astype(
        jnp.float32
    )
    list_terms = jnp.einsum("bn,bgj->ngj", select_a, atm_cells, precision=highest)
    owned = jnp.zeros((owned_blocks,) + list_terms.shape[1:], jnp.float32)
    for index in range(npairs):
        offset = owner_offset(index, npairs, ntile)
        back = passed_along(list_terms[2 * index : 2 * index + 2], "tile", offset)
        landing = (
            asked_list[index][:, None] == jnp.arange(owned_blocks, dtype=jnp.int32)[None, :]
        ).astype(jnp.float32)
        owned = owned + jnp.einsum("sa,sgc->agc", landing, back, precision=highest)
    totals = total_of_pieces(owned, "sub")
    nflux = totals.shape[1] - 1
    atm_flux = totals[:, :nflux] / jnp.maximum(totals[:, nflux:], 1.0)
    atm_flux = jnp.transpose(atm_flux, (1, 0, 2)).reshape(nflux, owned_blocks * blk)
    ocean_len = ocean_table.shape[0]
    select_o = (xb_ocn[:, None] == jnp.arange(ocean_len, dtype=jnp.int32)[None, :]).astype(
        jnp.float32
    )
    ocean_terms = jnp.einsum("bn,bgj->ngj", select_o, ocn_cells, precision=highest)
    ocean_mine = summed_on_arrival(ocean_terms, "sub", 0)
    ocn_flux = ocean_mine[:, :nflux] / jnp.maximum(ocean_mine[:, nflux:], 1.0)
    ocn_flux = jnp.transpose(ocn_flux, (1, 0, 2)).reshape(nflux, -1)
    return (atm_flux, ocn_flux)


def solution(mesh):
    placed = (
        P(None, ("member", "tile")),
        P(None, ("member", "tile", "sub")),
        P(("tile", "sub")),
        P(("tile", "sub")),
        P(("tile", "sub")),
        P(("tile", "sub")),
        P(("tile", "sub")),
        P(("tile", "sub")),
        P(("tile", "sub"), None, None),
        P(("tile", "sub"), None, None),
    )
    return jax.shard_map(
        per_device,
        mesh=mesh,
        in_specs=placed,
        out_specs=(P(None, ("member", "tile")), P(None, ("member", "tile", "sub"))),
        check_vma=False,
    )
```

profile of v0, /device:TPU:65, one launch (start us, length us, event | category | flops | bytes accessed | tf_op | source)
XLA Modules:
  0.0 175.1 jit_solution(11892738113145536841)
XLA Ops:
  3.5 42.9 %all-reduce = s32[16]{0:T(128)S(1)} all-reduce(s32[16]{0:T(128)S(1)} %dynamic-update-slice), channel_id=1, replica_groups=mesh['member'=2,'tile'=128,'sub'=2] {'sub'}, use_global_device_ids=true, to_apply=%add | all-reduce | flops 16 | bytes 128
  48.4 2.0 %collective-permute-start.12 = (s32[2]{0:T(128)S(1)}, s32[2]{0:T(128)S(1)}, u32[]{:S(2)}, u32[]{:S(2)}) collective-permute-start(s32[2]{0:T(128)S(1)} %get-tuple-element.22), channel_id=1, source_target_pairs={{250,0},{252,2},{254,4},{0,6},{2,8},{4,10},{6,12},{8,14},{10,16},{... | collective-permute-start | bytes 32 | tf_op jit(solution)/shard_map/ppermute | solution.py:10
  50.4 2.0 %collective-permute-start.10 = (s32[2]{0:T(128)S(1)}, s32[2]{0:T(128)S(1)}, u32[]{:S(2)}, u32[]{:S(2)}) collective-permute-start(s32[2]{0:T(128)S(1)} %get-tuple-element.23), channel_id=1, source_target_pairs={{252,0},{254,2},{0,4},{2,6},{4,8},{6,10},{8,12},{10,14},{12,16},{1... | collective-permute-start | bytes 32 | tf_op jit(solution)/shard_map/ppermute | solution.py:10
  52.4 2.0 %collective-permute-start.8 = (s32[2]{0:T(128)S(1)}, s32[2]{0:T(128)S(1)}, u32[]{:S(2)}, u32[]{:S(2)}) collective-permute-start(s32[2]{0:T(128)S(1)} %get-tuple-element.24), channel_id=1, source_target_pairs={{254,0},{0,2},{2,4},{4,6},{6,8},{8,10},{10,12},{12,14},{14,16},{16... | collective-permute-start | bytes 32 | tf_op jit(solution)/shard_map/ppermute | solution.py:10
  62.4 9.6 %collective-permute-start.4 = (s32[2]{0:T(128)S(1)}, s32[2]{0:T(128)S(1)}, u32[]{:S(2)}, u32[]{:S(2)}) collective-permute-start(s32[2]{0:T(128)S(1)} %get-tuple-element.26), channel_id=1, source_target_pairs={{2,0},{4,2},{6,4},{8,6},{10,8},{12,10},{14,12},{16,14},{18,16},{20... | collective-permute-start | bytes 32 | tf_op jit(solution)/shard_map/ppermute | solution.py:10
  72.0 4.6 %collective-permute-start.2 = (s32[2]{0:T(128)S(1)}, s32[2]{0:T(128)S(1)}, u32[]{:S(2)}, u32[]{:S(2)}) collective-permute-start(s32[2]{0:T(128)S(1)} %get-tuple-element.27), channel_id=1, source_target_pairs={{4,0},{6,2},{8,4},{10,6},{12,8},{14,10},{16,12},{18,14},{20,16},{2... | collective-permute-start | bytes 32 | tf_op jit(solution)/shard_map/ppermute | solution.py:10
  76.6 6.7 %collective-permute-start = (s32[2]{0:T(128)S(1)}, s32[2]{0:T(128)S(1)}, u32[]{:S(2)}, u32[]{:S(2)}) collective-permute-start(s32[2]{0:T(128)S(1)} %get-tuple-element.28), channel_id=1, source_target_pairs={{6,0},{8,2},{10,4},{12,6},{14,8},{16,10},{18,12},{20,14},{22,16},{... | collective-permute-start | bytes 32 | tf_op jit(solution)/shard_map/ppermute | solution.py:10
  90.5 2.1 %collective-permute-start.3 = (bf16[2,8,128]{2,1,0:T(8,128)(2,1)S(1)}, bf16[2,8,128]{2,1,0:T(8,128)(2,1)S(1)}, u32[]{:S(2)}, u32[]{:S(2)}) collective-permute-start(bf16[2,8,128]{2,1,0:T(8,128)(2,1)S(1)} %gather_fusion.1), channel_id=1, source_target_pairs={{252,0},{254,2},{0,4},{2,6},{4,8},{6,10},{8,12},{10,14},{12,16},{1... | collective-permute-start | bytes 12296 | tf_op jit(solution)/shard_map/ppermute | solution.py:10
  92.6 4.8 %collective-permute-start.5 = (bf16[2,8,128]{2,1,0:T(8,128)(2,1)S(1)}, bf16[2,8,128]{2,1,0:T(8,128)(2,1)S(1)}, u32[]{:S(2)}, u32[]{:S(2)}) collective-permute-start(bf16[2,8,128]{2,1,0:T(8,128)(2,1)S(1)} %gather_fusion.2), channel_id=1, source_target_pairs={{254,0},{0,2},{2,4},{4,6},{6,8},{8,10},{10,12},{12,14},{14,16},{16... | collective-permute-start | bytes 12296 | tf_op jit(solution)/shard_map/ppermute | solution.py:10
  97.5 3.8 %collective-permute-start.9 = (bf16[2,8,128]{2,1,0:T(8,128)(2,1)S(1)}, bf16[2,8,128]{2,1,0:T(8,128)(2,1)S(1)}, u32[]{:S(2)}, u32[]{:S(2)}) collective-permute-start(bf16[2,8,128]{2,1,0:T(8,128)(2,1)S(1)} %gather_fusion.4), channel_id=1, source_target_pairs={{2,0},{4,2},{6,4},{8,6},{10,8},{12,10},{14,12},{16,14},{18,16},{20... | collective-permute-start | bytes 12296 | tf_op jit(solution)/shard_map/ppermute | solution.py:10
  101.3 4.4 %collective-permute-start.11 = (bf16[2,8,128]{2,1,0:T(8,128)(2,1)S(1)}, bf16[2,8,128]{2,1,0:T(8,128)(2,1)S(1)}, u32[]{:S(2)}, u32[]{:S(2)}) collective-permute-start(bf16[2,8,128]{2,1,0:T(8,128)(2,1)S(1)} %gather_fusion.5), channel_id=1, source_target_pairs={{4,0},{6,2},{8,4},{10,6},{12,8},{14,10},{16,12},{18,14},{20,16},{2... | collective-permute-start | bytes 12296 | tf_op jit(solution)/shard_map/ppermute | solution.py:10
  105.7 6.4 %collective-permute-start.13 = (bf16[2,8,128]{2,1,0:T(8,128)(2,1)S(1)}, bf16[2,8,128]{2,1,0:T(8,128)(2,1)S(1)}, u32[]{:S(2)}, u32[]{:S(2)}) collective-permute-start(bf16[2,8,128]{2,1,0:T(8,128)(2,1)S(1)} %gather_fusion.6), channel_id=1, source_target_pairs={{6,0},{8,2},{10,4},{12,6},{14,8},{16,10},{18,12},{20,14},{22,16},{... | collective-permute-start | bytes 12296 | tf_op jit(solution)/shard_map/ppermute | solution.py:10
  112.2 5.0 %collective-permute-start.15 = (bf16[2,8,128]{2,1,0:T(8,128)(2,1)S(1)}, bf16[2,8,128]{2,1,0:T(8,128)(2,1)S(1)}, u32[]{:S(2)}, u32[]{:S(2)}) collective-permute-start(bf16[2,8,128]{2,1,0:T(8,128)(2,1)S(1)} %gather_fusion.7), channel_id=1, source_target_pairs={{128,0},{130,2},{132,4},{134,6},{136,8},{138,10},{140,12},{142,14}... | collective-permute-start | bytes 12296 | tf_op jit(solution)/shard_map/ppermute | solution.py:10
  117.3 3.2 %collective-permute-done.15 = bf16[2,8,128]{2,1,0:T(8,128)(2,1)S(1)} collective-permute-done((bf16[2,8,128]{2,1,0:T(8,128)(2,1)S(1)}, bf16[2,8,128]{2,1,0:T(8,128)(2,1)S(1)}, u32[]{:S(2)}, u32[]{:S(2)}) %collective-permute-start.15) | collective-permute-done | bytes 4128 | tf_op jit(solution)/shard_map/ppermute | solution.py:10
  122.4 6.4 %collective-permute-start.16 = (f32[2,5,128]{2,0,1:T(2,128)S(1)}, f32[2,5,128]{2,0,1:T(2,128)S(1)}, u32[]{:S(2)}, u32[]{:S(2)}) collective-permute-start(f32[2,5,128]{2,0,1:T(2,128)S(1)} %get-tuple-element.10), channel_id=1, source_target_pairs={{6,0},{8,2},{10,4},{12,6},{14,8},{16,10},{18,12},{20,14},{22,16},{... | collective-permute-start | bytes 15368 | tf_op jit(solution)/shard_map/ppermute | solution.py:10
  128.8 5.0 %collective-permute-start.23 = (f32[2,5,128]{2,0,1:T(2,128)S(1)}, f32[2,5,128]{2,0,1:T(2,128)S(1)}, u32[]{:S(2)}, u32[]{:S(2)}) collective-permute-start(f32[2,5,128]{2,0,1:T(2,128)S(1)} %get-tuple-element.11), channel_id=1, source_target_pairs={{128,0},{130,2},{132,4},{134,6},{136,8},{138,10},{140,12},{142,14}... | collective-permute-start | bytes 15368 | tf_op jit(solution)/shard_map/ppermute | solution.py:10
  133.8 2.0 %collective-permute-start.22 = (f32[2,5,128]{2,0,1:T(2,128)S(1)}, f32[2,5,128]{2,0,1:T(2,128)S(1)}, u32[]{:S(2)}, u32[]{:S(2)}) collective-permute-start(f32[2,5,128]{2,0,1:T(2,128)S(1)} %get-tuple-element.12), channel_id=1, source_target_pairs={{250,0},{252,2},{254,4},{0,6},{2,8},{4,10},{6,12},{8,14},{10,16},{... | collective-permute-start | bytes 15368 | tf_op jit(solution)/shard_map/ppermute | solution.py:10
  135.7 2.0 %collective-permute-start.21 = (f32[2,5,128]{2,0,1:T(2,128)S(1)}, f32[2,5,128]{2,0,1:T(2,128)S(1)}, u32[]{:S(2)}, u32[]{:S(2)}) collective-permute-start(f32[2,5,128]{2,0,1:T(2,128)S(1)} %get-tuple-element.13), channel_id=1, source_target_pairs={{252,0},{254,2},{0,4},{2,6},{4,8},{6,10},{8,12},{10,14},{12,16},{1... | collective-permute-start | bytes 15368 | tf_op jit(solution)/shard_map/ppermute | solution.py:10
  137.7 7.6 %collective-permute-start.17 = (f32[2,5,128]{2,0,1:T(2,128)S(1)}, f32[2,5,128]{2,0,1:T(2,128)S(1)}, u32[]{:S(2)}, u32[]{:S(2)}) collective-permute-start(f32[2,5,128]{2,0,1:T(2,128)S(1)} %get-tuple-element.17), channel_id=1, source_target_pairs={{4,0},{6,2},{8,4},{10,6},{12,8},{14,10},{16,12},{18,14},{20,16},{2... | collective-permute-start | bytes 15368 | tf_op jit(solution)/shard_map/ppermute | solution.py:10
  146.2 9.4 %all_to_all.5 = f32[2,8,5,128]{3,1,2,0:T(8,128)S(1)} all-to-all(f32[2,8,5,128]{3,1,2,0:T(8,128)S(1)} %copy.23), channel_id=1, replica_groups=mesh['member'=2,'tile'=128,'sub'=2] {'sub'}, dimensions={0} | all-to-all | bytes 81920 | tf_op jit(solution)/shard_map/all_to_all | solution.py:25
  156.3 3.1 %collective-permute-start.18 = (f32[2,5,128]{2,0,1:T(2,128)S(1)}, f32[2,5,128]{2,0,1:T(2,128)S(1)}, u32[]{:S(2)}, u32[]{:S(2)}) collective-permute-start(f32[2,5,128]{2,0,1:T(2,128)S(1)} %get-tuple-element.16), channel_id=1, source_target_pairs={{2,0},{4,2},{6,4},{8,6},{10,8},{12,10},{14,12},{16,14},{18,16},{20... | collective-permute-start | bytes 15368 | tf_op jit(solution)/shard_map/ppermute | solution.py:10
  161.0 2.2 %collective-permute-start.20 = (f32[2,5,128]{2,0,1:T(2,128)S(1)}, f32[2,5,128]{2,0,1:T(2,128)S(1)}, u32[]{:S(2)}, u32[]{:S(2)}) collective-permute-start(f32[2,5,128]{2,0,1:T(2,128)S(1)} %get-tuple-element.14), channel_id=1, source_target_pairs={{254,0},{0,2},{2,4},{4,6},{6,8},{8,10},{10,12},{12,14},{14,16},{16... | collective-permute-start | bytes 15368 | tf_op jit(solution)/shard_map/ppermute | solution.py:10
  163.5 5.2 %collective-permute-done.20 = f32[2,5,128]{2,0,1:T(2,128)S(1)} collective-permute-done((f32[2,5,128]{2,0,1:T(2,128)S(1)}, f32[2,5,128]{2,0,1:T(2,128)S(1)}, u32[]{:S(2)}, u32[]{:S(2)}) %collective-permute-start.20) | collective-permute-done | bytes 5152 | tf_op jit(solution)/shard_map/ppermute | solution.py:10
  170.2 4.2 %all-gather = f32[32,5,128]{2,0,1:T(8,128)S(1)} all-gather(f32[16,5,128]{2,0,1:T(8,128)S(1)} %fusion.5), channel_id=2, replica_groups=mesh['member'=2,'tile'=128,'sub'=2] {'sub'}, dimensions={0}, use_global_device_ids=true | all-gather | bytes 122880 | tf_op jit(solution)/shard_map/all_gather | solution.py:14
  (118 shorter events, 26.0 us)
Async XLA Ops:
  46.5 15.9 %collective-permute-start.14 = (s32[2]{0:T(128)S(1)}, s32[2]{0:T(128)S(1)}, u32[]{:S(2)}, u32[]{:S(2)}) collective-permute-start(s32[2]{0:T(128)S(1)} %get-tuple-element.21), channel_id=1, source_target_pairs={{128,0},{130,2},{132,4},{134,6},{136,8},{138,10},{140,12},{142,14}... | collective-permute-start | bytes 32 | tf_op jit(solution)/shard_map/ppermute | solution.py:10
  48.4 23.6 %collective-permute-start.12 = (s32[2]{0:T(128)S(1)}, s32[2]{0:T(128)S(1)}, u32[]{:S(2)}, u32[]{:S(2)}) collective-permute-start(s32[2]{0:T(128)S(1)} %get-tuple-element.22), channel_id=1, source_target_pairs={{250,0},{252,2},{254,4},{0,6},{2,8},{4,10},{6,12},{8,14},{10,16},{... | collective-permute-start | bytes 32 | tf_op jit(solution)/shard_map/ppermute | solution.py:10
  50.4 26.2 %collective-permute-start.10 = (s32[2]{0:T(128)S(1)}, s32[2]{0:T(128)S(1)}, u32[]{:S(2)}, u32[]{:S(2)}) collective-permute-start(s32[2]{0:T(128)S(1)} %get-tuple-element.23), channel_id=1, source_target_pairs={{252,0},{254,2},{0,4},{2,6},{4,8},{6,10},{8,12},{10,14},{12,16},{1... | collective-permute-start | bytes 32 | tf_op jit(solution)/shard_map/ppermute | solution.py:10
  52.4 31.0 %collective-permute-start.8 = (s32[2]{0:T(128)S(1)}, s32[2]{0:T(128)S(1)}, u32[]{:S(2)}, u32[]{:S(2)}) collective-permute-start(s32[2]{0:T(128)S(1)} %get-tuple-element.24), channel_id=1, source_target_pairs={{254,0},{0,2},{2,4},{4,6},{6,8},{8,10},{10,12},{12,14},{14,16},{16... | collective-permute-start | bytes 32 | tf_op jit(solution)/shard_map/ppermute | solution.py:10
  54.3 29.1 %collective-permute-start.6 = (s32[2]{0:T(128)S(1)}, s32[2]{0:T(128)S(1)}, u32[]{:S(2)}, u32[]{:S(2)}) collective-permute-start(s32[2]{0:T(128)S(1)} %get-tuple-element.25), channel_id=1, source_target_pairs={{0,0},{2,2},{4,4},{6,6},{8,8},{10,10},{12,12},{14,14},{16,16},{18,... | collective-permute-start | bytes 32 | tf_op jit(solution)/shard_map/ppermute | solution.py:10
  62.4 21.0 %collective-permute-start.4 = (s32[2]{0:T(128)S(1)}, s32[2]{0:T(128)S(1)}, u32[]{:S(2)}, u32[]{:S(2)}) collective-permute-start(s32[2]{0:T(128)S(1)} %get-tuple-element.26), channel_id=1, source_target_pairs={{2,0},{4,2},{6,4},{8,6},{10,8},{12,10},{14,12},{16,14},{18,16},{20... | collective-permute-start | bytes 32 | tf_op jit(solution)/shard_map/ppermute | solution.py:10
  72.0 14.5 %collective-permute-start.2 = (s32[2]{0:T(128)S(1)}, s32[2]{0:T(128)S(1)}, u32[]{:S(2)}, u32[]{:S(2)}) collective-permute-start(s32[2]{0:T(128)S(1)} %get-tuple-element.27), channel_id=1, source_target_pairs={{4,0},{6,2},{8,4},{10,6},{12,8},{14,10},{16,12},{18,14},{20,16},{2... | collective-permute-start | bytes 32 | tf_op jit(solution)/shard_map/ppermute | solution.py:10
  76.6 7.4 %collective-permute-start = (s32[2]{0:T(128)S(1)}, s32[2]{0:T(128)S(1)}, u32[]{:S(2)}, u32[]{:S(2)}) collective-permute-start(s32[2]{0:T(128)S(1)} %get-tuple-element.28), channel_id=1, source_target_pairs={{6,0},{8,2},{10,4},{12,6},{14,8},{16,10},{18,12},{20,14},{22,16},{... | collective-permute-start | bytes 32 | tf_op jit(solution)/shard_map/ppermute | solution.py:10
  84.6 16.7 %collective-permute-start.1 = (bf16[2,8,128]{2,1,0:T(8,128)(2,1)S(1)}, bf16[2,8,128]{2,1,0:T(8,128)(2,1)S(1)}, u32[]{:S(2)}, u32[]{:S(2)}) collective-permute-start(bf16[2,8,128]{2,1,0:T(8,128)(2,1)S(1)} %gather_fusion), channel_id=1, source_target_pairs={{250,0},{252,2},{254,4},{0,6},{2,8},{4,10},{6,12},{8,14},{10,16},{... | collective-permute-start | bytes 12296 | tf_op jit(solution)/shard_map/ppermute | solution.py:10
  90.5 15.2 %collective-permute-start.3 = (bf16[2,8,128]{2,1,0:T(8,128)(2,1)S(1)}, bf16[2,8,128]{2,1,0:T(8,128)(2,1)S(1)}, u32[]{:S(2)}, u32[]{:S(2)}) collective-permute-start(bf16[2,8,128]{2,1,0:T(8,128)(2,1)S(1)} %gather_fusion.1), channel_id=1, source_target_pairs={{252,0},{254,2},{0,4},{2,6},{4,8},{6,10},{8,12},{10,14},{12,16},{1... | collective-permute-start | bytes 12296 | tf_op jit(solution)/shard_map/ppermute | solution.py:10
  92.6 19.6 %collective-permute-start.5 = (bf16[2,8,128]{2,1,0:T(8,128)(2,1)S(1)}, bf16[2,8,128]{2,1,0:T(8,128)(2,1)S(1)}, u32[]{:S(2)}, u32[]{:S(2)}) collective-permute-start(bf16[2,8,128]{2,1,0:T(8,128)(2,1)S(1)} %gather_fusion.2), channel_id=1, source_target_pairs={{254,0},{0,2},{2,4},{4,6},{6,8},{8,10},{10,12},{12,14},{14,16},{16... | collective-permute-start | bytes 12296 | tf_op jit(solution)/shard_map/ppermute | solution.py:10
  97.5 19.7 %collective-permute-start.7 = (bf16[2,8,128]{2,1,0:T(8,128)(2,1)S(1)}, bf16[2,8,128]{2,1,0:T(8,128)(2,1)S(1)}, u32[]{:S(2)}, u32[]{:S(2)}) collective-permute-start(bf16[2,8,128]{2,1,0:T(8,128)(2,1)S(1)} %gather_fusion.3), channel_id=1, source_target_pairs={{0,0},{2,2},{4,4},{6,6},{8,8},{10,10},{12,12},{14,14},{16,16},{18,... | collective-permute-start | bytes 12296 | tf_op jit(solution)/shard_map/ppermute | solution.py:10
  97.5 19.7 %collective-permute-start.9 = (bf16[2,8,128]{2,1,0:T(8,128)(2,1)S(1)}, bf16[2,8,128]{2,1,0:T(8,128)(2,1)S(1)}, u32[]{:S(2)}, u32[]{:S(2)}) collective-permute-start(bf16[2,8,128]{2,1,0:T(8,128)(2,1)S(1)} %gather_fusion.4), channel_id=1, source_target_pairs={{2,0},{4,2},{6,4},{8,6},{10,8},{12,10},{14,12},{16,14},{18,16},{20... | collective-permute-start | bytes 12296 | tf_op jit(solution)/shard_map/ppermute | solution.py:10
  101.3 15.9 %collective-permute-start.11 = (bf16[2,8,128]{2,1,0:T(8,128)(2,1)S(1)}, bf16[2,8,128]{2,1,0:T(8,128)(2,1)S(1)}, u32[]{:S(2)}, u32[]{:S(2)}) collective-permute-start(bf16[2,8,128]{2,1,0:T(8,128)(2,1)S(1)} %gather_fusion.5), channel_id=1, source_target_pairs={{4,0},{6,2},{8,4},{10,6},{12,8},{14,10},{16,12},{18,14},{20,16},{2... | collective-permute-start | bytes 12296 | tf_op jit(solution)/shard_map/ppermute | solution.py:10
  105.7 11.5 %collective-permute-start.13 = (bf16[2,8,128]{2,1,0:T(8,128)(2,1)S(1)}, bf16[2,8,128]{2,1,0:T(8,128)(2,1)S(1)}, u32[]{:S(2)}, u32[]{:S(2)}) collective-permute-start(bf16[2,8,128]{2,1,0:T(8,128)(2,1)S(1)} %gather_fusion.6), channel_id=1, source_target_pairs={{6,0},{8,2},{10,4},{12,6},{14,8},{16,10},{18,12},{20,14},{22,16},{... | collective-permute-start | bytes 12296 | tf_op jit(solution)/shard_map/ppermute | solution.py:10
  112.2 8.3 %collective-permute-start.15 = (bf16[2,8,128]{2,1,0:T(8,128)(2,1)S(1)}, bf16[2,8,128]{2,1,0:T(8,128)(2,1)S(1)}, u32[]{:S(2)}, u32[]{:S(2)}) collective-permute-start(bf16[2,8,128]{2,1,0:T(8,128)(2,1)S(1)} %gather_fusion.7), channel_id=1, source_target_pairs={{128,0},{130,2},{132,4},{134,6},{136,8},{138,10},{140,12},{142,14}... | collective-permute-start | bytes 12296 | tf_op jit(solution)/shard_map/ppermute | solution.py:10
  122.4 47.5 %collective-permute-start.16 = (f32[2,5,128]{2,0,1:T(2,128)S(1)}, f32[2,5,128]{2,0,1:T(2,128)S(1)}, u32[]{:S(2)}, u32[]{:S(2)}) collective-permute-start(f32[2,5,128]{2,0,1:T(2,128)S(1)} %get-tuple-element.10), channel_id=1, source_target_pairs={{6,0},{8,2},{10,4},{12,6},{14,8},{16,10},{18,12},{20,14},{22,16},{... | collective-permute-start | bytes 15368 | tf_op jit(solution)/shard_map/ppermute | solution.py:10
  128.8 40.8 %collective-permute-start.23 = (f32[2,5,128]{2,0,1:T(2,128)S(1)}, f32[2,5,128]{2,0,1:T(2,128)S(1)}, u32[]{:S(2)}, u32[]{:S(2)}) collective-permute-start(f32[2,5,128]{2,0,1:T(2,128)S(1)} %get-tuple-element.11), channel_id=1, source_target_pairs={{128,0},{130,2},{132,4},{134,6},{136,8},{138,10},{140,12},{142,14}... | collective-permute-start | bytes 15368 | tf_op jit(solution)/shard_map/ppermute | solution.py:10
  133.8 35.5 %collective-permute-start.22 = (f32[2,5,128]{2,0,1:T(2,128)S(1)}, f32[2,5,128]{2,0,1:T(2,128)S(1)}, u32[]{:S(2)}, u32[]{:S(2)}) collective-permute-start(f32[2,5,128]{2,0,1:T(2,128)S(1)} %get-tuple-element.12), channel_id=1, source_target_pairs={{250,0},{252,2},{254,4},{0,6},{2,8},{4,10},{6,12},{8,14},{10,16},{... | collective-permute-start | bytes 15368 | tf_op jit(solution)/shard_map/ppermute | solution.py:10
  135.7 33.3 %collective-permute-start.21 = (f32[2,5,128]{2,0,1:T(2,128)S(1)}, f32[2,5,128]{2,0,1:T(2,128)S(1)}, u32[]{:S(2)}, u32[]{:S(2)}) collective-permute-start(f32[2,5,128]{2,0,1:T(2,128)S(1)} %get-tuple-element.13), channel_id=1, source_target_pairs={{252,0},{254,2},{0,4},{2,6},{4,8},{6,10},{8,12},{10,14},{12,16},{1... | collective-permute-start | bytes 15368 | tf_op jit(solution)/shard_map/ppermute | solution.py:10
  137.7 18.6 %collective-permute-start.17 = (f32[2,5,128]{2,0,1:T(2,128)S(1)}, f32[2,5,128]{2,0,1:T(2,128)S(1)}, u32[]{:S(2)}, u32[]{:S(2)}) collective-permute-start(f32[2,5,128]{2,0,1:T(2,128)S(1)} %get-tuple-element.17), channel_id=1, source_target_pairs={{4,0},{6,2},{8,4},{10,6},{12,8},{14,10},{16,12},{18,14},{20,16},{2... | collective-permute-start | bytes 15368 | tf_op jit(solution)/shard_map/ppermute | solution.py:10
  156.3 4.4 %collective-permute-start.18 = (f32[2,5,128]{2,0,1:T(2,128)S(1)}, f32[2,5,128]{2,0,1:T(2,128)S(1)}, u32[]{:S(2)}, u32[]{:S(2)}) collective-permute-start(f32[2,5,128]{2,0,1:T(2,128)S(1)} %get-tuple-element.16), channel_id=1, source_target_pairs={{2,0},{4,2},{6,4},{8,6},{10,8},{12,10},{14,12},{16,14},{18,16},{20... | collective-permute-start | bytes 15368 | tf_op jit(solution)/shard_map/ppermute | solution.py:10
  160.7 0.3 collective-permute-start.19
  161.0 7.7 %collective-permute-start.20 = (f32[2,5,128]{2,0,1:T(2,128)S(1)}, f32[2,5,128]{2,0,1:T(2,128)S(1)}, u32[]{:S(2)}, u32[]{:S(2)}) collective-permute-start(f32[2,5,128]{2,0,1:T(2,128)S(1)} %get-tuple-element.14), channel_id=1, source_target_pairs={{254,0},{0,2},{2,4},{4,6},{6,8},{8,10},{10,12},{12,14},{14,16},{16... | collective-permute-start | bytes 15368 | tf_op jit(solution)/shard_map/ppermute | solution.py:10
  (6 other events, 202.7 us)
where the time goes:
time: 176 us; the launch traced here: 175 us
  starting transfers between devices  85.4 us (49%)
  blocking collectives  58.4 us (33%)
  local copies, waits for them, and re-layouts  10.4 us (6%)
  waiting for transfers between devices  9.99 us (6%)
  other arithmetic  4.33 us (2%)
  matrix products  3.88 us (2%)
  between operations  2.65 us (2%)
    ppermute x24, starting transfers between devices, passed_along(): return lax.ppermute(block, axis, route)  85.4 us
    unnamed x1, blocking collectives  42.9 us
    ppermute x24, waiting for transfers between devices, passed_along(): return lax.ppermute(block, axis, route)  9.99 us
    all_to_all x1, blocking collectives, summed_on_arrival(): lax.all_to_all(in_blocks(array, dim, length), axis, 0, 0, tiled=True)  9.43 us
    unnamed x24, local copies, waits for them, and re-layouts  4.71 us
    gather x8, local copies, waits for them, and re-layouts, per_device(): reply = passed_along(table[asked], 'tile', -offset)  4.47 us
    all_gather x1, blocking collectives, total_of_pieces(): return lax.all_gather(array, axis).sum(0)  4.21 us
  transfers between devices with their start and end apart: 24, of which 4 were waited for; matrix products, arithmetic and copies ran while one was open for 7% of the time, Pallas kernels for 0%

commit v1 on v0

v1 whole, which is shorter than its diff:
```python
import functools

import jax
import jax.numpy as jnp
from jax import lax
from jax.experimental import pallas as pl
from jax.experimental.pallas import tpu as pltpu
from jax.sharding import PartitionSpec as P

MESH = pl.DeviceIdType.MESH
F32 = jnp.float32
BF16 = jnp.bfloat16


def owner_offset(index, npairs, ntile):
    if index < npairs - 1:
        return index - npairs // 2 + 1
    return ntile // 2


def dot_nt(left, right):
    return lax.dot_general(left, right, (((1,), (1,)), ((), ())), preferred_element_type=F32)


def dot_nn(left, right):
    return jnp.dot(left, right, preferred_element_type=F32)


def split(value):
    high = value.astype(BF16).astype(F32)
    return high, value - high


def bulk_fluxes(ta, qa, ua, va, ps, sw, lw, pr, sst, uo, vo, albedo):
    du = ua - uo
    dv = va - vo
    factor = (0.3 + 0.1 * jnp.tanh(ps)) * jnp.sqrt(du * du + dv * dv + 1.0)
    sens = factor * (sst - ta)
    lat = factor * (0.5 * sst - qa)
    taux = factor * du
    tauy = factor * dv
    heat = (1.0 - albedo) * sw + lw - 0.2 * sst - sens - lat
    fresh = pr - 0.5 * lat
    return (sens, lat, taux, tauy), (heat, taux, tauy, fresh)


def kernel(
    ntile,
    npairs,
    atm_hbm,
    ocn_hbm,
    need_hbm,
    xneed_hbm,
    xocn_hbm,
    count_hbm,
    sea_hbm,
    area_hbm,
    wa_hbm,
    wo_hbm,
    atm_out,
    ocn_out,
    need_s,
    xneed_s,
    xocn_s,
    count_s,
    table,
    ocean,
    sea_v,
    area_v,
    wa,
    wo,
    field_a,
    field_o,
    sums_a,
    terms,
    note_out,
    note_in,
    place,
    inverse,
    back_out,
    back_in,
    sea_out,
    sea_in,
    local_sem,
    list_sem,
    ocean_sem,
    push_send,
    push_recv,
    pass_send,
    pass_recv,
    note_send,
    note_recv,
    back_send,
    back_recv,
    final_sem,
):
    tile = lax.axis_index("tile")
    core = lax.axis_index("sub")
    other = 1 - core
    nblocks, blk = wa.shape[0], wa.shape[2]
    owned = table.shape[0] // npairs
    part = owned // 2
    mine = npairs // 2 - 1
    order = [i for i in sorted(range(npairs), key=lambda i: -abs(owner_offset(i, npairs, ntile))) if i != mine]

    def asker(index):
        return lax.rem(tile + 2 * ntile - owner_offset(index, npairs, ntile), ntile)

    def owner(index):
        return lax.rem(tile + ntile + owner_offset(index, npairs, ntile), ntile)

    def remote(source, target, send, recv, where):
        return pltpu.make_async_remote_copy(
            src_ref=source, dst_ref=target, send_sem=send, recv_sem=recv, device_id=where, device_id_type=MESH
        )

    barrier = pltpu.get_barrier_semaphore()
    for index in order:
        for side in range(2):
            pl.semaphore_signal(barrier, inc=1, device_id={"tile": owner(index), "sub": side}, device_id_type=MESH)
    pl.semaphore_signal(barrier, inc=1, device_id={"sub": other}, device_id_type=MESH)

    sources = (atm_hbm, need_hbm, ocn_hbm, xneed_hbm, xocn_hbm, count_hbm, sea_hbm, area_hbm, wa_hbm, wo_hbm)
    targets = (
        table.at[pl.ds(mine * owned, owned)],
        need_s.at[core],
        ocean.at[pl.ds(core * part, part)],
        xneed_s,
        xocn_s,
        count_s,
        sea_v,
        area_v,
        wa,
        wo,
    )
    local = [
        pltpu.make_async_copy(source, target, local_sem.at[i])
        for i, (source, target) in enumerate(zip(sources, targets))
    ]
    for copy in local:
        copy.start()
    local[0].wait()
    local[1].wait()
    local[2].wait()
    pl.semaphore_wait(barrier, 2 * len(order) + 1)

    pushes = {}
    for index in order:
        pushes[index] = remote(
            table.at[pl.ds(mine * owned + core * part, part)],
            table.at[pl.ds(index * owned + core * part, part)],
            push_send.at[index],
            push_recv.at[index],
            {"tile": asker(index)},
        )
        pushes[index].start()
    lists = remote(need_s.at[core], need_s.at[core], list_sem.at[0], list_sem.at[1], {"sub": other})
    lists.start()
    waters = remote(
        ocean.at[pl.ds(core * part, part)],
        ocean.at[pl.ds(core * part, part)],
        ocean_sem.at[0],
        ocean_sem.at[1],
        {"sub": other},
    )
    waters.start()
    for copy in local[3:]:
        copy.wait()

    rows = lax.broadcasted_iota(jnp.int32, (8, blk), 0)
    live = (lax.broadcasted_iota(jnp.int32, (nblocks, blk), 0) < count_s[0]).astype(F32)
    weighted = area_v[...] * live
    wet = weighted * sea_v[...].astype(F32)

    high, low = split(weighted)
    near = jnp.zeros((8, blk), F32)
    far = jnp.zeros((8, blk), F32)
    for b in range(nblocks):
        left = jnp.concatenate(
            [jnp.broadcast_to(high[b : b + 1], (8, blk)), jnp.broadcast_to(low[b : b + 1], (8, blk))], 0
        ).astype(BF16)
        cells = dot_nn(left, wa[b])
        cells = cells[:8] + cells[8:]
        near = near + jnp.where(rows == xneed_s[b], cells, 0.0)
        far = far + jnp.where(rows + 8 == xneed_s[b], cells, 0.0)
    lists.wait()
    for index in range(npairs):
        held = near if index < npairs // 2 else far
        at = (2 * index) % 8
        note_out[index, 0:2] = held[at : at + 2]
        for k in range(2):
            entry = 2 * index + k
            local_block = need_s[entry // 8, entry % 8] & (owned - 1)
            note_out[index, 2 + k : 3 + k] = jnp.full((1, blk), local_block, jnp.int32).astype(F32)
    notes = {}
    for index in order:
        for side in range(2):
            notes[index, side] = remote(
                note_out.at[index],
                note_in.at[index, core],
                note_send.at[index, side],
                note_recv.at[index, core],
                {"tile": owner(index), "sub": side},
            )
            notes[index, side].start()
    note_near = remote(
        note_out.at[mine],
        note_in.at[mine, core],
        note_send.at[mine, 0],
        note_recv.at[mine, core],
        {"sub": other},
    )
    note_near.start()
    note_in[mine, core] = note_out[mine]

    waters.wait()
    for b in range(nblocks):
        state = ocean[xocn_s[b]].astype(F32)
        left = jnp.concatenate([state, jnp.ones((8 - state.shape[0], blk), F32)], 0).astype(BF16)
        field_o[b] = dot_nt(left, wo[b])
    for b in range(nblocks):
        sums_a[b] = dot_nt(jnp.ones((8, blk), BF16), wa[b])
    per_ocean = 1.0 / field_o[:, 4, :]
    per_atm = 1.0 / sums_a[:, 0, :]
    sst = field_o[:, 0, :] * per_ocean
    uo = field_o[:, 1, :] * per_ocean
    vo = field_o[:, 2, :] * per_ocean
    albedo = 0.06 + 0.1 * jax.nn.sigmoid(field_o[:, 3, :] * per_ocean)

    passes = {}
    for index in order:
        pushes[index].wait_recv()
        half = table.at[pl.ds(index * owned + core * part, part)]
        passes[index] = remote(half, half, pass_send.at[index], pass_recv.at[index], {"sub": other})
        passes[index].start()
    for index in order:
        passes[index].wait_recv()

    for b in range(nblocks):
        entry = xneed_s[b]
        block = need_s[entry >> 3, entry & 7] & (owned - 1)
        field_a[b] = dot_nt(table[(entry >> 1) * owned + block], wa[b])
    states = [field_a[:, f, :] * per_atm for f in range(8)]
    to_atm, to_ocn = bulk_fluxes(*states, sst, uo, vo, albedo)
    for g in range(4):
        high, low = split(to_atm[g] * wet)
        terms[:, g, :] = high
        terms[:, g + 4, :] = high
        terms[:, g + 8, :] = low
        terms[:, g + 12, :] = low
    lower = (rows >= 4).astype(jnp.int32)
    pairs = [jnp.zeros((8, blk), F32) for _ in range(npairs)]
    for b in range(nblocks):
        cells = dot_nn(terms[b].astype(BF16), wa[b])
        cells = cells[:8] + cells[8:]
        entry = xneed_s[b] - lower
        for index in range(npairs):
            pairs[index] = pairs[index] + jnp.where(entry == 2 * index, cells, 0.0)
    for index in range(npairs):
        back_out[index] = pairs[index]
    backs = {}
    for index in order:
        for side in range(2):
            backs[index, side] = remote(
                back_out.at[index],
                back_in.at[index, core],
                back_send.at[index, side],
                back_recv.at[index, core],
                {"tile": owner(index), "sub": side},
            )
            backs[index, side].start()
    back_near = remote(
        back_out.at[mine],
        back_in.at[mine, core],
        back_send.at[mine, 0],
        back_recv.at[mine, core],
        {"sub": other},
    )
    back_near.start()
    back_in[mine, core] = pairs[mine]

    for g in range(5):
        high, low = split(to_ocn[g] * wet if g < 4 else wet)
        terms[:, g, :] = high
        terms[:, g + 8, :] = low
    for g in range(5, 8):
        terms[:, g, :] = jnp.zeros((nblocks, blk), F32)
        terms[:, g + 8, :] = jnp.zeros((nblocks, blk), F32)
    sums = [jnp.zeros((8, blk), F32) for _ in range(2 * part)]
    for b in range(nblocks):
        cells = dot_nn(terms[b].astype(BF16), wo[b])
        cells = cells[:8] + cells[8:]
        entry = jnp.full((8, blk), xocn_s[b], jnp.int32)
        for index in range(2 * part):
            sums[index] = sums[index] + jnp.where(entry == index, cells, 0.0)
    for index in range(2 * part):
        sea_out[index // part, index % part] = sums[index]
    shore = remote(sea_out.at[other], sea_in, final_sem.at[0], final_sem.at[1], {"sub": other})
    shore.start()

    for index in order:
        for side in range(2):
            remote(
                note_out.at[index],
                note_in.at[index, side],
                note_send.at[index, side],
                note_recv.at[index, side],
                {"tile": owner(index), "sub": side},
            ).wait_recv()
    remote(
        note_out.at[mine],
        note_in.at[mine, other],
        note_send.at[mine, 0],
        note_recv.at[mine, other],
        {"sub": other},
    ).wait_recv()
    areas = []
    spots = []
    for index in range(npairs):
        areas.append(note_in[index, 0, 0:2] + note_in[index, 1, 0:2])
        spot = note_in[index, 0, 2:4]
        spots.append(spot)
        place[index] = jnp.concatenate(
            [jnp.broadcast_to(spot[0:1], (4, blk)), jnp.broadcast_to(spot[1:2], (4, blk))], 0
        )
    areas = jnp.concatenate(areas, 0)
    spots = jnp.concatenate(spots, 0)
    for a in range(owned):
        total = jnp.sum(jnp.where(spots == float(a), areas, 0.0), 0, keepdims=True)
        inverse[a : a + 1] = 1.0 / jnp.maximum(total, 1.0)

    shore.wait_recv()
    for m in range(part):
        total = sea_out[core, m] + sea_in[m]
        ocn_out[m] = total[:4] / jnp.maximum(total[4:5], 1.0)

    for index in order:
        for side in range(2):
            remote(
                back_out.at[index],
                back_in.at[index, side],
                back_send.at[index, side],
                back_recv.at[index, side],
                {"tile": owner(index), "sub": side},
            ).wait_recv()
    remote(
        back_out.at[mine],
        back_in.at[mine, other],
        back_send.at[mine, 0],
        back_recv.at[mine, other],
        {"sub": other},
    ).wait_recv()
    pairs = [back_in[index, 0] + back_in[index, 1] for index in range(npairs)]
    for a in range(owned):
        total = jnp.zeros((8, blk), F32)
        for index in range(npairs):
            total = total + jnp.where(place[index] == float(a), pairs[index], 0.0)
        atm_out[a] = (total[:4] + total[4:]) * inverse[a : a + 1]

    for index in order:
        pushes[index].wait_send()
        passes[index].wait_send()
        for side in range(2):
            notes[index, side].wait_send()
            backs[index, side].wait_send()
    note_near.wait_send()
    back_near.wait_send()
    shore.wait_send()


def per_device(atm_state, ocn_state, need_atm, xb_need, xb_ocn, xb_count, sea_mask, cell_area, w_atm, w_ocn):
    ntile = lax.axis_size("tile")
    fields_a = atm_state.shape[0]
    fields_o = ocn_state.shape[0]
    nblocks, blk = w_atm.shape[0], w_atm.shape[1]
    npairs = need_atm.shape[0]
    owned = atm_state.shape[1] // blk
    waters = ocn_state.shape[1] // blk
    nflux = 4
    atm = jnp.transpose(atm_state.reshape(fields_a, owned, blk), (1, 0, 2))
    ocn = jnp.transpose(ocn_state.reshape(fields_o, waters, blk), (1, 0, 2))
    dma = pltpu.SemaphoreType.DMA
    vmem = pltpu.VMEM
    atm_flux, ocn_flux = pl.pallas_call(
        functools.partial(kernel, ntile, npairs),
        out_shape=(
            jax.ShapeDtypeStruct((owned, nflux, blk), F32),
            jax.ShapeDtypeStruct((waters, nflux, blk), F32),
        ),
        in_specs=[pl.BlockSpec(memory_space=pl.ANY)] * 10,
        out_specs=[pl.BlockSpec(memory_space=pltpu.VMEM)] * 2,
        scratch_shapes=[
            pltpu.SMEM((2, npairs), jnp.int32),
            pltpu.SMEM((nblocks,), jnp.int32),
            pltpu.SMEM((nblocks,), jnp.int32),
            pltpu.SMEM((1,), jnp.int32),
            vmem((npairs * owned, fields_a, blk), BF16),
            vmem((2 * waters, fields_o, blk), BF16),
            vmem((nblocks, blk), jnp.int32),
            vmem((nblocks, blk), F32),
            vmem((nblocks, blk, blk), BF16),
            vmem((nblocks, blk, blk), BF16),
            vmem((nblocks, 8, blk), F32),
            vmem((nblocks, 8, blk), F32),
            vmem((nblocks, 8, blk), F32),
            vmem((nblocks, 16, blk), F32),
            vmem((npairs, 4, blk), F32),
            vmem((npairs, 2, 4, blk), F32),
            vmem((npairs, 8, blk), F32),
            vmem((owned, blk), F32),
            vmem((npairs, 8, blk), F32),
            vmem((npairs, 2, 8, blk), F32),
            vmem((2, waters, 8, blk), F32),
            vmem((waters, 8, blk), F32),
            dma((10,)),
            dma((2,)),
            dma((2,)),
            dma((npairs,)),
            dma((npairs,)),
            dma((npairs,)),
            dma((npairs,)),
            dma((npairs, 2)),
            dma((npairs, 2)),
            dma((npairs, 2)),
            dma((npairs, 2)),
            dma((2,)),
        ],
        compiler_params=pltpu.CompilerParams(collective_id=0, has_side_effects=True),
    )(
        atm,
        ocn,
        need_atm,
        xb_need,
        xb_ocn,
        xb_count,
        sea_mask.reshape(nblocks, blk),
        cell_area.reshape(nblocks, blk),
        w_atm,
        w_ocn,
    )
    atm_flux = jnp.transpose(atm_flux, (1, 0, 2)).reshape(nflux, owned * blk)
    ocn_flux = jnp.transpose(ocn_flux, (1, 0, 2)).reshape(nflux, waters * blk)
    return (atm_flux, ocn_flux)


def solution(mesh):
    placed = (
        P(None, ("member", "tile")),
        P(None, ("member", "tile", "sub")),
        P(("tile", "sub")),
        P(("tile", "sub")),
        P(("tile", "sub")),
        P(("tile", "sub")),
        P(("tile", "sub")),
        P(("tile", "sub")),
        P(("tile", "sub"), None, None),
        P(("tile", "sub"), None, None),
    )
    return jax.shard_map(
        per_device,
        mesh=mesh,
        in_specs=placed,
        out_specs=(P(None, ("member", "tile")), P(None, ("member", "tile", "sub"))),
        check_vma=False,
    )
```

time: 176 us -> 64.6 us (0.37)
  starting transfers between devices: 85.4 us -> 0 us
  Pallas kernels: 0 us -> 61.1 us
  blocking collectives: 58.4 us -> 0 us
  waiting for transfers between devices: 9.99 us -> 0 us
  local copies, waits for them, and re-layouts: 10.4 us -> 1.99 us
  other arithmetic: 4.33 us -> 0 us
  matrix products: 3.88 us -> 0 us
    ppermute x24 -> x0, starting transfers between devices: 85.4 us -> none  [passed_along(): return lax.ppermute(block, axis, route)]
    pallas_call x0 -> x1, Pallas kernels: none -> 61.1 us  [per_device(): pl.pallas_call(functools.partial(kernel, ntile, npairs), out_shape=(jax.S...]
    unnamed x1 -> x0, blocking collectives: 42.9 us -> none
    ppermute x24 -> x0, waiting for transfers between devices: 9.99 us -> none  [passed_along(): return lax.ppermute(block, axis, route)]
    all_to_all x1 -> x0, blocking collectives: 9.43 us -> none  [summed_on_arrival(): lax.all_to_all(in_blocks(array, dim, length), axis, 0, 0, tiled=True)]
    all_gather x2 -> x0, blocking collectives: 6.05 us -> none  [the longest x1 4.21 us: total_of_pieces(): return lax.all_gather(array, axis).sum(0)]
    gather x10 -> x0, local copies, waits for them, and re-layouts: 5.61 us -> none  [the longest x8 4.47 us: per_device(): reply = passed_along(table[asked], 'tile', -offset)]
    dot_general x14 -> x0, matrix products: 3.88 us -> none  [the longest x8 2.25 us: per_device(): owned = owned + jnp.einsum('sa,sgc->agc', landing, back, precision=highest)]
  transfers between devices with their start and end apart: 24 -> 0, of which waited for: 4 -> 0; matrix products, arithmetic and copies ran while one was open for 7% -> 0% of each run, Pallas kernels for 0% -> 0%
where the time goes in v1:
time: 64.6 us; the launch traced here: 64.4 us
  Pallas kernels  61.1 us (95%)
  local copies, waits for them, and re-layouts  1.99 us (3%)
  between operations  1.3 us (2%)
    pallas_call x1, Pallas kernels, per_device(): pl.pallas_call(functools.partial(kernel, ntile, npairs), out_shape=(jax.S...  61.1 us
    unnamed x4, local copies, waits for them, and re-layouts  1.99 us

profile of v1, /device:TPU:65, one launch (start us, length us, event | category | flops | bytes accessed | tf_op | source)
XLA Modules:
  0.0 64.4 jit_solution(6053048581852635011)
XLA Ops:
  1.3 61.1 %shard_map.113 = (f32[16,4,128]{2,1,0:T(4,128)}, f32[8,4,128]{2,1,0:T(4,128)}) custom-call(bf16[16,8,128]{2,1,0:T(8,128)(2,1)} %bitcast.14, bf16[8,4,128]{2,1,0:T(4,128)(2,1)} %bitcast.17, s32[8]{0:T(128)} %need_hbm.1, s32[8]{0:T(128)} %xneed_hbm.1, s32[8]{0:T(128)} %xocn_hbm.1, s32[1]{0:T(128)S(6)} %copy.14.count_hbm, s32[8,128]{1,0:T(8,128)} %bitcast.18, ...), custom_call_target="tpu_custom_call" | custom-call | tf_op jit(solution)/shard_map/pallas_call | solution.py:384
  62.4 0.0 copy-start
  62.4 1.4 %copy.15 = f32[4,2048]{1,0:T(4,128)} copy(f32[4,2048]{1,0:T(4,128)} %bitcast.15) | data formatting | bytes 65536
  63.8 0.0 copy-done
  63.8 0.6 copy.16
Async XLA Ops:
  62.4 1.4 %copy-start = (f32[8,4,128]{2,1,0:T(4,128)S(1)}, f32[8,4,128]{2,1,0:T(4,128)}, u32[]{:S(2)}) copy-start(f32[8,4,128]{2,1,0:T(4,128)} %get-tuple-element.5) | copy-start | bytes 49156

commit v2 on v1

--- a/solution.py
+++ b/solution.py
@@ -10,6 +10,8 @@
 MESH = pl.DeviceIdType.MESH
 F32 = jnp.float32
 BF16 = jnp.bfloat16
+VMEM_LIMIT = 60 << 20
+LANDING_LIMIT = 4 << 20
 
 
 def owner_offset(index, npairs, ntile):
@@ -57,7 +59,9 @@
     area_hbm,
     wa_hbm,
     wo_hbm,
-    atm_out,
+    back_in,
+    place,
+    inverse,
     ocn_out,
     need_s,
     xneed_s,
@@ -75,10 +79,7 @@
     terms,
     note_out,
     note_in,
-    place,
-    inverse,
     back_out,
-    back_in,
     sea_out,
     sea_in,
     local_sem,
@@ -350,12 +351,6 @@
         back_recv.at[mine, other],
         {"sub": other},
     ).wait_recv()
-    pairs = [back_in[index, 0] + back_in[index, 1] for index in range(npairs)]
-    for a in range(owned):
-        total = jnp.zeros((8, blk), F32)
-        for index in range(npairs):
-            total = total + jnp.where(place[index] == float(a), pairs[index], 0.0)
-        atm_out[a] = (total[:4] + total[4:]) * inverse[a : a + 1]
 
     for index in order:
         pushes[index].wait_send()
@@ -366,6 +361,17 @@
     note_near.wait_send()
     back_near.wait_send()
     shore.wait_send()
+
+
+def landing(back, place, inverse, ocean, atm_out, ocn_out):
+    npairs = back.shape[0]
+    pairs = [back[index, 0] + back[index, 1] for index in range(npairs)]
+    for a in range(inverse.shape[0]):
+        total = jnp.zeros(pairs[0].shape, F32)
+        for index in range(npairs):
+            total = total + jnp.where(place[index] == float(a), pairs[index], 0.0)
+        atm_out[a] = (total[:4] + total[4:]) * inverse[a : a + 1]
+    ocn_out[...] = ocean[...]
 
 
 def per_device(atm_state, ocn_state, need_atm, xb_need, xb_ocn, xb_count, sea_mask, cell_area, w_atm, w_ocn):
@@ -381,14 +387,17 @@
     ocn = jnp.transpose(ocn_state.reshape(fields_o, waters, blk), (1, 0, 2))
     dma = pltpu.SemaphoreType.DMA
     vmem = pltpu.VMEM
-    atm_flux, ocn_flux = pl.pallas_call(
+    in_vmem = pl.BlockSpec(memory_space=vmem)
+    arrived = pl.pallas_call(
         functools.partial(kernel, ntile, npairs),
         out_shape=(
-            jax.ShapeDtypeStruct((owned, nflux, blk), F32),
-            jax.ShapeDtypeStruct((waters, nflux, blk), F32),
+            vmem((npairs, 2, 8, blk), F32),
+            vmem((npairs, 8, blk), F32),
+            vmem((owned, blk), F32),
+            vmem((waters, nflux, blk), F32),
         ),
         in_specs=[pl.BlockSpec(memory_space=pl.ANY)] * 10,
-        out_specs=[pl.BlockSpec(memory_space=pltpu.VMEM)] * 2,
+        out_specs=[in_vmem] * 4,
         scratch_shapes=[
             pltpu.SMEM((2, npairs), jnp.int32),
             pltpu.SMEM((nblocks,), jnp.int32),
@@ -407,9 +416,6 @@
             vmem((npairs, 4, blk), F32),
             vmem((npairs, 2, 4, blk), F32),
             vmem((npairs, 8, blk), F32),
-            vmem((owned, blk), F32),
-            vmem((npairs, 8, blk), F32),
-            vmem((npairs, 2, 8, blk), F32),
             vmem((2, waters, 8, blk), F32),
             vmem((waters, 8, blk), F32),
             dma((10,)),
@@ -425,7 +431,9 @@
             dma((npairs, 2)),
             dma((2,)),
         ],
-        compiler_params=pltpu.CompilerParams(collective_id=0, has_side_effects=True),
+        compiler_params=pltpu.CompilerParams(
+            collective_id=0, has_side_effects=True, vmem_limit_bytes=VMEM_LIMIT
+        ),
     )(
         atm,
         ocn,
@@ -438,6 +446,16 @@
         w_atm,
         w_ocn,
     )
+    atm_flux, ocn_flux = pl.pallas_call(
+        landing,
+        out_shape=(
+            jax.ShapeDtypeStruct((owned, nflux, blk), F32),
+            jax.ShapeDtypeStruct((waters, nflux, blk), F32),
+        ),
+        in_specs=[in_vmem] * 4,
+        out_specs=[in_vmem] * 2,
+        compiler_params=pltpu.CompilerParams(vmem_limit_bytes=LANDING_LIMIT),
+    )(*arrived)
     atm_flux = jnp.transpose(atm_flux, (1, 0, 2)).reshape(nflux, owned * blk)
     ocn_flux = jnp.transpose(ocn_flux, (1, 0, 2)).reshape(nflux, waters * blk)
     return (atm_flux, ocn_flux)

time: 64.6 us -> 62.6 us (0.969)
  local copies, waits for them, and re-layouts: 1.99 us -> 0 us
    unnamed x4 -> x0, local copies, waits for them, and re-layouts: 1.99 us -> none
    pallas_call x1 -> x2, Pallas kernels: 61.1 us -> 61.1 us  [the longest x1 60.4 us: per_device(): pl.pallas_call(functools.partial(kernel, ntile, npairs), out_shape=(vmem(...]
where the time goes in v2:
time: 62.6 us; the launch traced here: 62.4 us
  Pallas kernels  61.1 us (98%)
  between operations  1.29 us (2%)
    pallas_call x1, Pallas kernels, per_device(): pl.pallas_call(functools.partial(kernel, ntile, npairs), out_shape=(vmem(...  60.4 us

profile of v2, /device:TPU:65, one launch (start us, length us, event | category | flops | bytes accessed | tf_op | source)
XLA Modules:
  0.0 62.4 jit_solution(4211846668305359833)
XLA Ops:
  1.3 60.4 %shard_map.113 = (f32[8,2,8,128]{3,2,1,0:T(8,128)S(1)}, f32[8,8,128]{2,1,0:T(8,128)S(1)}, f32[16,128]{1,0:T(8,128)S(1)}, f32[8,4,128]{2,1,0:T(4,128)S(1)}) custom-call(bf16[16,8,128]{2,1,0:T(8,128)(2,1)} %bitcast.14, bf16[8,4,128]{2,1,0:T(4,128)(2,1)} %bitcast.15, s32[8]{0:T(128)} %need_hbm.1, s32[8]{0:T(128)} %xneed_hbm.1, s32[8]{0:T(128)} %xocn_hbm.1, ...), custom_call_target="tpu_custom_call" | custom-call | tf_op jit(solution)/shard_map/pallas_call | solution.py:391
  61.7 0.7 %shard_map.114 = (f32[16,4,128]{2,1,0:T(4,128)}, f32[8,4,128]{2,1,0:T(4,128)}) custom-call(f32[8,2,8,128]{3,2,1,0:T(8,128)S(1)} %get-tuple-element.8.back, f32[8,8,128]{2,1,0:T(8,128)S(1)} %get-tuple-element.9.place, f32[16,128]{1,0:T(8,128)S(1)} %get-tuple-element.10.inverse, f32[8,4,128]{2,1,0:T(4,128)S(1)} %get-tuple-element.11.ocean), custom_call_target="tpu_custom_call" | custom-call | tf_op jit(solution)/shard_map/pallas_call | solution.py:449

commit v3 on v0

v3 whole, which is shorter than its diff:
```python
import functools

import jax
import jax.numpy as jnp
from jax import lax
from jax.experimental import pallas as pl
from jax.experimental.pallas import tpu as pltpu
from jax.sharding import PartitionSpec as P

MESH = pl.DeviceIdType.MESH
F32 = jnp.float32
BF16 = jnp.bfloat16
VMEM_LIMIT = 60 << 20
LANDING_LIMIT = 4 << 20


def owner_offset(index, npairs, ntile):
    if index < npairs - 1:
        return index - npairs // 2 + 1
    return ntile // 2


def dot_nt(left, right):
    return lax.dot_general(left, right, (((1,), (1,)), ((), ())), preferred_element_type=F32)


def dot_nn(left, right):
    return jnp.dot(left, right, preferred_element_type=F32)


def split(value):
    high = value.astype(BF16).astype(F32)
    return high, value - high


def bulk_fluxes(ta, qa, ua, va, ps, sw, lw, pr, sst, uo, vo, albedo):
    du = ua - uo
    dv = va - vo
    factor = (0.3 + 0.1 * jnp.tanh(ps)) * jnp.sqrt(du * du + dv * dv + 1.0)
    sens = factor * (sst - ta)
    lat = factor * (0.5 * sst - qa)
    taux = factor * du
    tauy = factor * dv
    heat = (1.0 - albedo) * sw + lw - 0.2 * sst - sens - lat
    fresh = pr - 0.5 * lat
    return (sens, lat, taux, tauy), (heat, taux, tauy, fresh)


def all_of(ref, sem):
    return pltpu.make_async_copy(ref, ref, sem)


def kernel(
    ntile,
    npairs,
    atm_hbm,
    ocn_hbm,
    need_hbm,
    xneed_hbm,
    xocn_hbm,
    count_hbm,
    sea_hbm,
    area_hbm,
    wa_hbm,
    wo_hbm,
    back_in,
    place,
    inverse,
    ocn_out,
    index_s,
    count_s,
    table,
    ocean,
    sea_v,
    area_v,
    wa,
    wo,
    field_a,
    field_o,
    sums_a,
    terms,
    note_out,
    note_in,
    back_out,
    shore,
    local_sem,
    gift_send,
    gift_recv,
    push_sem,
    note_sem,
    back_sem,
    prep_sem,
):
    tile = lax.axis_index("tile")
    core = lax.axis_index("sub")
    nblocks, blk = wa.shape[0], wa.shape[2]
    half = nblocks // 2
    owned = table.shape[0] // npairs
    mine = npairs // 2 - 1
    order = [i for i in sorted(range(npairs), key=lambda i: -abs(owner_offset(i, npairs, ntile))) if i != mine]
    there = len(order)

    def asker(index):
        return lax.rem(tile + 2 * ntile - owner_offset(index, npairs, ntile), ntile)

    def owner(index):
        return lax.rem(tile + ntile + owner_offset(index, npairs, ntile), ntile)

    def remote(source, target, send, recv, where):
        return pltpu.make_async_remote_copy(
            src_ref=source, dst_ref=target, send_sem=send, recv_sem=recv, device_id=where, device_id_type=MESH
        )

    barrier = pltpu.get_barrier_semaphore()
    lists = (need_hbm, xneed_hbm, xocn_hbm)
    small = ((ocn_hbm, ocean), (sea_hbm, sea_v), (area_hbm, area_v))
    large = ((wa_hbm, wa), (wo_hbm, wo))

    def slot(ref, side):
        return ref.at[pl.ds(side * half, half)]

    @pl.when(core == 0)
    def _():
        pl.semaphore_signal(barrier, inc=1, device_id={"sub": 1}, device_id_type=MESH)
        for row, source in enumerate(lists):
            pltpu.make_async_copy(source, index_s.at[0, row], local_sem.at[1]).start()
        count = pltpu.make_async_copy(count_hbm, count_s.at[0], local_sem.at[2])
        count.start()
        pl.semaphore_wait(barrier, 1)
        for source, target in large:
            remote(source, slot(target, 0), gift_send.at[3], gift_recv.at[3], {"sub": 1}).start()
        for source, target in small:
            remote(source, slot(target, 0), gift_send.at[2], gift_recv.at[2], {"sub": 1}).start()
        all_of(index_s.at[0], local_sem.at[1]).wait()
        count.wait()
        numbers = remote(index_s.at[0], index_s.at[0], gift_send.at[0], gift_recv.at[0], {"sub": 1})
        numbers.start()
        limit = remote(count_s.at[0], count_s.at[0], gift_send.at[1], gift_recv.at[1], {"sub": 1})
        limit.start()
        numbers.wait_send()
        limit.wait_send()
        all_of(ocean, gift_send.at[2]).wait()
        all_of(wa, gift_send.at[3]).wait()
        all_of(field_a.at[pl.ds(0, 14)], prep_sem.at[1]).wait()
        all_of(back_in, back_sem.at[1]).wait()

    @pl.when(core == 1)
    def _():
        for index in order:
            pl.semaphore_signal(barrier, inc=1, device_id={"tile": owner(index)}, device_id_type=MESH)
        pl.semaphore_signal(barrier, inc=1, device_id={"sub": 0}, device_id_type=MESH)
        home = pltpu.make_async_copy(atm_hbm, table.at[pl.ds(mine * owned, owned)], local_sem.at[0])
        home.start()
        for row, source in enumerate(lists):
            pltpu.make_async_copy(source, index_s.at[1, row], local_sem.at[1]).start()
        count = pltpu.make_async_copy(count_hbm, count_s.at[1], local_sem.at[2])
        count.start()
        for source, target in small:
            pltpu.make_async_copy(source, slot(target, 1), local_sem.at[3]).start()
        for source, target in large:
            pltpu.make_async_copy(source, slot(target, 1), local_sem.at[4]).start()
        home.wait()
        pl.semaphore_wait(barrier, there + 1)
        for index in order:
            remote(
                table.at[pl.ds(mine * owned, owned)],
                table.at[pl.ds(index * owned, owned)],
                push_sem.at[0],
                push_sem.at[1],
                {"tile": asker(index)},
            ).start()
        all_of(index_s.at[1], local_sem.at[1]).wait()
        count.wait()
        all_of(ocean, local_sem.at[3]).wait()
        all_of(wa, local_sem.at[4]).wait()
        all_of(index_s.at[0], gift_recv.at[0]).wait()
        all_of(count_s.at[0], gift_recv.at[1]).wait()
        all_of(ocean, gift_recv.at[2]).wait()
        all_of(wa, gift_recv.at[3]).wait()

        def listed(entry):
            return index_s[entry >> 3, 0, entry & 7] & (owned - 1)

        xneed = [index_s[b // half, 1, b % half] for b in range(nblocks)]
        xocn = [index_s[b // half, 2, b % half] for b in range(nblocks)]
        rows = lax.broadcasted_iota(jnp.int32, (8, blk), 0)
        block = lax.broadcasted_iota(jnp.int32, (nblocks, blk), 0)
        live = (block < jnp.where(block < half, count_s[0, 0], half + count_s[1, 0])).astype(F32)
        weighted = area_v[...] * live
        wet = weighted * sea_v[...].astype(F32)

        high, low = split(weighted)
        near = jnp.zeros((8, blk), F32)
        far = jnp.zeros((8, blk), F32)
        for b in range(nblocks):
            left = jnp.concatenate(
                [jnp.broadcast_to(high[b : b + 1], (8, blk)), jnp.broadcast_to(low[b : b + 1], (8, blk))], 0
            ).astype(BF16)
            cells = dot_nn(left, wa[b])
            cells = cells[:8] + cells[8:]
            near = near + jnp.where(rows == xneed[b], cells, 0.0)
            far = far + jnp.where(rows + 8 == xneed[b], cells, 0.0)
        for index in range(npairs):
            held = near if index < npairs // 2 else far
            at = (2 * index) % 8
            note_out[index, 0:2] = held[at : at + 2]
            for k in range(2):
                note_out[index, 2 + k : 3 + k] = jnp.full((1, blk), listed(2 * index + k), jnp.int32).astype(F32)
        for index in order:
            remote(
                note_out.at[index], note_in.at[index], note_sem.at[0], note_sem.at[1], {"tile": owner(index)}
            ).start()

        for b in range(nblocks):
            state = ocean[xocn[b]].astype(F32)
            left = jnp.concatenate([state, jnp.ones((8 - state.shape[0], blk), F32)], 0).astype(BF16)
            field_o[b] = dot_nt(left, wo[b])
        for b in range(nblocks):
            sums_a[b] = dot_nt(jnp.ones((8, blk), BF16), wa[b])
        per_ocean = 1.0 / field_o[:, 4, :]
        per_atm = 1.0 / sums_a[:, 0, :]
        sst = field_o[:, 0, :] * per_ocean
        uo = field_o[:, 1, :] * per_ocean
        vo = field_o[:, 2, :] * per_ocean
        albedo = 0.06 + 0.1 * jax.nn.sigmoid(field_o[:, 3, :] * per_ocean)
        spots = [xneed[b] >> 1 for b in range(nblocks)]
        spots = [spots[b] * owned + listed(xneed[b]) for b in range(nblocks)]

        all_of(table.at[pl.ds(0, there * owned)], push_sem.at[1]).wait()
        for b in range(nblocks):
            field_a[b] = dot_nt(table[spots[b]], wa[b])
        states = [field_a[:, f, :] * per_atm for f in range(8)]
        to_atm, to_ocn = bulk_fluxes(*states, sst, uo, vo, albedo)
        for g in range(4):
            high, low = split(to_atm[g] * wet)
            terms[:, g, :] = high
            terms[:, g + 4, :] = high
            terms[:, g + 8, :] = low
            terms[:, g + 12, :] = low
        lower = (rows >= 4).astype(jnp.int32)
        pairs = [jnp.zeros((8, blk), F32) for _ in range(npairs)]
        for b in range(nblocks):
            cells = dot_nn(terms[b].astype(BF16), wa[b])
            cells = cells[:8] + cells[8:]
            entry = xneed[b] - lower
            for index in range(npairs):
                pairs[index] = pairs[index] + jnp.where(entry == 2 * index, cells, 0.0)
        for index in range(npairs):
            back_out[index] = pairs[index]
        for index in order:
            for side in (0, 1):
                remote(
                    back_out.at[index],
                    back_in.at[index],
                    back_sem.at[0],
                    back_sem.at[1],
                    {"tile": owner(index), "sub": side},
                ).start()
        remote(back_out.at[mine], back_in.at[mine], back_sem.at[0], back_sem.at[1], {"sub": 0}).start()
        back_in[mine] = pairs[mine]

        all_of(note_in.at[pl.ds(0, there)], note_sem.at[1]).wait()
        areas = []
        places = []
        for index in range(npairs):
            note = note_out[index] if index == mine else note_in[index]
            areas.append(note[0:2])
            places.append(note[2:4])
            place[index] = jnp.concatenate(
                [jnp.broadcast_to(note[2:3], (4, blk)), jnp.broadcast_to(note[3:4], (4, blk))], 0
            )
        areas = jnp.concatenate(areas, 0)
        places = jnp.concatenate(places, 0)
        for a in range(owned):
            total = jnp.sum(jnp.where(places == float(a), areas, 0.0), 0, keepdims=True)
            inverse[a : a + 1] = 1.0 / jnp.maximum(total, 1.0)
        remote(place, place, prep_sem.at[0], prep_sem.at[1], {"sub": 0}).start()
        remote(inverse, inverse, prep_sem.at[0], prep_sem.at[1], {"sub": 0}).start()
        for g in range(5):
            high, low = split(to_ocn[g] * wet if g < 4 else wet)
            terms[:, g, :] = high
            terms[:, g + 8, :] = low
        for g in range(5, 8):
            terms[:, g, :] = jnp.zeros((nblocks, blk), F32)
            terms[:, g + 8, :] = jnp.zeros((nblocks, blk), F32)
        sums = [jnp.zeros((8, blk), F32) for _ in range(2 * half)]
        for b in range(nblocks):
            cells = dot_nn(terms[b].astype(BF16), wo[b])
            cells = cells[:8] + cells[8:]
            entry = jnp.full((8, blk), xocn[b], jnp.int32)
            for index in range(2 * half):
                sums[index] = sums[index] + jnp.where(entry == index, cells, 0.0)
        for index in range(2 * half):
            flux = sums[index][:4] / jnp.maximum(sums[index][4:5], 1.0)
            if index < half:
                shore[index] = flux
            else:
                ocn_out[index - half] = flux
        remote(shore, ocn_out, prep_sem.at[0], prep_sem.at[1], {"sub": 0}).start()

        all_of(table.at[pl.ds(0, there * owned)], push_sem.at[0]).wait()
        all_of(note_out.at[pl.ds(0, there)], note_sem.at[0]).wait()
        all_of(back_in.at[pl.ds(0, there)], back_sem.at[1]).wait()
        all_of(field_a.at[pl.ds(0, 2 * there + 1)], back_sem.at[0]).wait()
        all_of(field_a.at[pl.ds(0, 14)], prep_sem.at[0]).wait()


def landing(back, place, inverse, ocean, atm_out, ocn_out):
    npairs = back.shape[0]
    pairs = [back[index] for index in range(npairs)]
    for a in range(inverse.shape[0]):
        total = jnp.zeros(pairs[0].shape, F32)
        for index in range(npairs):
            total = total + jnp.where(place[index] == float(a), pairs[index], 0.0)
        atm_out[a] = (total[:4] + total[4:]) * inverse[a : a + 1]
    ocn_out[...] = ocean[...]


def per_device(atm_state, ocn_state, need_atm, xb_need, xb_ocn, xb_count, sea_mask, cell_area, w_atm, w_ocn):
    ntile = lax.axis_size("tile")
    fields_a = atm_state.shape[0]
    fields_o = ocn_state.shape[0]
    nblocks, blk = w_atm.shape[0], w_atm.shape[1]
    npairs = need_atm.shape[0]
    owned = atm_state.shape[1] // blk
    waters = ocn_state.shape[1] // blk
    nflux = 4
    atm = jnp.transpose(atm_state.reshape(fields_a, owned, blk), (1, 0, 2))
    ocn = jnp.transpose(ocn_state.reshape(fields_o, waters, blk), (1, 0, 2))
    dma = pltpu.SemaphoreType.DMA
    vmem = pltpu.VMEM
    in_vmem = pl.BlockSpec(memory_space=vmem)
    arrived = pl.pallas_call(
        functools.partial(kernel, ntile, npairs),
        out_shape=(
            vmem((npairs, 8, blk), F32),
            vmem((npairs, 8, blk), F32),
            vmem((owned, blk), F32),
            vmem((waters, nflux, blk), F32),
        ),
        in_specs=[pl.BlockSpec(memory_space=pl.ANY)] * 10,
        out_specs=[in_vmem] * 4,
        scratch_shapes=[
            pltpu.SMEM((2, 3, npairs), jnp.int32),
            pltpu.SMEM((2, 1), jnp.int32),
            vmem((npairs * owned, fields_a, blk), BF16),
            vmem((2 * waters, fields_o, blk), BF16),
            vmem((2 * nblocks, blk), jnp.int32),
            vmem((2 * nblocks, blk), F32),
            vmem((2 * nblocks, blk, blk), BF16),
            vmem((2 * nblocks, blk, blk), BF16),
            vmem((2 * nblocks, 8, blk), F32),
            vmem((2 * nblocks, 8, blk), F32),
            vmem((2 * nblocks, 8, blk), F32),
            vmem((2 * nblocks, 16, blk), F32),
            vmem((npairs, 4, blk), F32),
            vmem((npairs, 4, blk), F32),
            vmem((npairs, 8, blk), F32),
            vmem((waters, nflux, blk), F32),
            dma((5,)),
            dma((4,)),
            dma((4,)),
            dma((2,)),
            dma((2,)),
            dma((2,)),
            dma((2,)),
        ],
        compiler_params=pltpu.CompilerParams(
            collective_id=0, has_side_effects=True, vmem_limit_bytes=VMEM_LIMIT
        ),
    )(
        atm,
        ocn,
        need_atm,
        xb_need,
        xb_ocn,
        xb_count,
        sea_mask.reshape(nblocks, blk),
        cell_area.reshape(nblocks, blk),
        w_atm,
        w_ocn,
    )
    atm_flux, ocn_flux = pl.pallas_call(
        landing,
        out_shape=(
            jax.ShapeDtypeStruct((owned, nflux, blk), F32),
            jax.ShapeDtypeStruct((waters, nflux, blk), F32),
        ),
        in_specs=[in_vmem] * 4,
        out_specs=[in_vmem] * 2,
        compiler_params=pltpu.CompilerParams(vmem_limit_bytes=LANDING_LIMIT),
    )(*arrived)
    atm_flux = jnp.transpose(atm_flux, (1, 0, 2)).reshape(nflux, owned * blk)
    ocn_flux = jnp.transpose(ocn_flux, (1, 0, 2)).reshape(nflux, waters * blk)
    return (atm_flux, ocn_flux)


def solution(mesh):
    placed = (
        P(None, ("member", "tile")),
        P(None, ("member", "tile", "sub")),
        P(("tile", "sub")),
        P(("tile", "sub")),
        P(("tile", "sub")),
        P(("tile", "sub")),
        P(("tile", "sub")),
        P(("tile", "sub")),
        P(("tile", "sub"), None, None),
        P(("tile", "sub"), None, None),
    )
    return jax.shard_map(
        per_device,
        mesh=mesh,
        in_specs=placed,
        out_specs=(P(None, ("member", "tile")), P(None, ("member", "tile", "sub"))),
        check_vma=False,
    )
```

time: 176 us -> 59.5 us (0.34)
  starting transfers between devices: 85.4 us -> 0 us
  blocking collectives: 58.4 us -> 0 us
  Pallas kernels: 0 us -> 58.1 us
  local copies, waits for them, and re-layouts: 10.4 us -> 0 us
  waiting for transfers between devices: 9.99 us -> 0 us
  other arithmetic: 4.33 us -> 0 us
  matrix products: 3.88 us -> 0 us
    ppermute x24 -> x0, starting transfers between devices: 85.4 us -> none  [passed_along(): return lax.ppermute(block, axis, route)]
    pallas_call x0 -> x2, Pallas kernels: none -> 58.1 us  [the longest x1 57.4 us: per_device(): pl.pallas_call(functools.partial(kernel, ntile, npairs), out_shape=(vmem(...]
    unnamed x1 -> x0, blocking collectives: 42.9 us -> none
    ppermute x24 -> x0, waiting for transfers between devices: 9.99 us -> none  [passed_along(): return lax.ppermute(block, axis, route)]
    all_to_all x1 -> x0, blocking collectives: 9.43 us -> none  [summed_on_arrival(): lax.all_to_all(in_blocks(array, dim, length), axis, 0, 0, tiled=True)]
    all_gather x2 -> x0, blocking collectives: 6.05 us -> none  [the longest x1 4.21 us: total_of_pieces(): return lax.all_gather(array, axis).sum(0)]
    gather x10 -> x0, local copies, waits for them, and re-layouts: 5.61 us -> none  [the longest x8 4.47 us: per_device(): reply = passed_along(table[asked], 'tile', -offset)]
    unnamed x24 -> x0, local copies, waits for them, and re-layouts: 4.71 us -> none
  transfers between devices with their start and end apart: 24 -> 0, of which waited for: 4 -> 0; matrix products, arithmetic and copies ran while one was open for 7% -> 0% of each run, Pallas kernels for 0% -> 0%
where the time goes in v3:
time: 59.5 us; the launch traced here: 59.4 us
  Pallas kernels  58.1 us (98%)
  between operations  1.29 us (2%)
    pallas_call x1, Pallas kernels, per_device(): pl.pallas_call(functools.partial(kernel, ntile, npairs), out_shape=(vmem(...  57.4 us

profile of v3, /device:TPU:65, one launch (start us, length us, event | category | flops | bytes accessed | tf_op | source)
XLA Modules:
  0.0 59.4 jit_solution(13484304333409140294)
XLA Ops:
  1.3 57.4 %shard_map.113 = (f32[8,8,128]{2,1,0:T(8,128)S(1)}, f32[8,8,128]{2,1,0:T(8,128)S(1)}, f32[16,128]{1,0:T(8,128)S(1)}, f32[8,4,128]{2,1,0:T(4,128)S(1)}) custom-call(bf16[16,8,128]{2,1,0:T(8,128)(2,1)} %bitcast.14, bf16[8,4,128]{2,1,0:T(4,128)(2,1)} %bitcast.15, s32[8]{0:T(128)} %need_hbm.1, s32[8]{0:T(128)} %xneed_hbm.1, s32[8]{0:T(128)} %xocn_hbm.1, ...), custom_call_target="tpu_custom_call" | custom-call | tf_op jit(solution)/shard_map/pallas_call | solution.py:333
  58.7 0.7 %shard_map.114 = (f32[16,4,128]{2,1,0:T(4,128)}, f32[8,4,128]{2,1,0:T(4,128)}) custom-call(f32[8,8,128]{2,1,0:T(8,128)S(1)} %get-tuple-element.8.back, f32[8,8,128]{2,1,0:T(8,128)S(1)} %get-tuple-element.9.place, f32[16,128]{1,0:T(8,128)S(1)} %get-tuple-element.10.inverse, f32[8,4,128]{2,1,0:T(4,128)S(1)} %get-tuple-element.11.ocean), custom_call_target="tpu_custom_call" | custom-call | tf_op jit(solution)/shard_map/pallas_call | solution.py:383

commit v4 on v3

--- a/solution.py
+++ b/solution.py
@@ -75,6 +75,7 @@
     area_v,
     wa,
     wo,
+    turned,
     field_a,
     field_o,
     sums_a,
@@ -97,8 +98,11 @@
     half = nblocks // 2
     owned = table.shape[0] // npairs
     mine = npairs // 2 - 1
-    order = [i for i in sorted(range(npairs), key=lambda i: -abs(owner_offset(i, npairs, ntile))) if i != mine]
-    there = len(order)
+    above = list(range(mine + 1, npairs - 1))
+    below = list(range(mine))
+    far_first = above[::-1] + [npairs - 1] + below
+    near_first = above + [npairs - 1] + below[::-1]
+    there = len(far_first)
 
     def asker(index):
         return lax.rem(tile + 2 * ntile - owner_offset(index, npairs, ntile), ntile)
@@ -141,12 +145,12 @@
         limit.wait_send()
         all_of(ocean, gift_send.at[2]).wait()
         all_of(wa, gift_send.at[3]).wait()
-        all_of(field_a.at[pl.ds(0, 14)], prep_sem.at[1]).wait()
+        all_of(field_a.at[pl.ds(0, 8 * 14)], prep_sem.at[1]).wait()
         all_of(back_in, back_sem.at[1]).wait()
 
     @pl.when(core == 1)
     def _():
-        for index in order:
+        for index in far_first:
             pl.semaphore_signal(barrier, inc=1, device_id={"tile": owner(index)}, device_id_type=MESH)
         pl.semaphore_signal(barrier, inc=1, device_id={"sub": 0}, device_id_type=MESH)
         home = pltpu.make_async_copy(atm_hbm, table.at[pl.ds(mine * owned, owned)], local_sem.at[0])
@@ -161,7 +165,7 @@
             pltpu.make_async_copy(source, slot(target, 1), local_sem.at[4]).start()
         home.wait()
         pl.semaphore_wait(barrier, there + 1)
-        for index in order:
+        for index in far_first:
             remote(
                 table.at[pl.ds(mine * owned, owned)],
                 table.at[pl.ds(index * owned, owned)],
@@ -178,6 +182,9 @@
         all_of(ocean, gift_recv.at[2]).wait()
         all_of(wa, gift_recv.at[3]).wait()
 
+        def every(first, stride):
+            return pl.ds(first, nblocks, stride=stride), slice(None)
+
         def listed(entry):
             return index_s[entry >> 3, 0, entry & 7] & (owned - 1)
 
@@ -206,7 +213,7 @@
             note_out[index, 0:2] = held[at : at + 2]
             for k in range(2):
                 note_out[index, 2 + k : 3 + k] = jnp.full((1, blk), listed(2 * index + k), jnp.int32).astype(F32)
-        for index in order:
+        for index in far_first:
             remote(
                 note_out.at[index], note_in.at[index], note_sem.at[0], note_sem.at[1], {"tile": owner(index)}
             ).start()
@@ -214,40 +221,41 @@
         for b in range(nblocks):
             state = ocean[xocn[b]].astype(F32)
             left = jnp.concatenate([state, jnp.ones((8 - state.shape[0], blk), F32)], 0).astype(BF16)
-            field_o[b] = dot_nt(left, wo[b])
-        for b in range(nblocks):
-            sums_a[b] = dot_nt(jnp.ones((8, blk), BF16), wa[b])
-        per_ocean = 1.0 / field_o[:, 4, :]
-        per_atm = 1.0 / sums_a[:, 0, :]
-        sst = field_o[:, 0, :] * per_ocean
-        uo = field_o[:, 1, :] * per_ocean
-        vo = field_o[:, 2, :] * per_ocean
-        albedo = 0.06 + 0.1 * jax.nn.sigmoid(field_o[:, 3, :] * per_ocean)
+            field_o[8 * b : 8 * b + 8] = dot_nt(left, wo[b])
+        for b in range(nblocks):
+            turned[b] = wa[b].T
+            sums_a[8 * b : 8 * b + 8] = dot_nn(jnp.ones((8, blk), BF16), turned[b])
+        per_ocean = 1.0 / field_o[every(4, 8)]
+        per_atm = 1.0 / sums_a[every(0, 8)]
+        sst = field_o[every(0, 8)] * per_ocean
+        uo = field_o[every(1, 8)] * per_ocean
+        vo = field_o[every(2, 8)] * per_ocean
+        albedo = 0.06 + 0.1 * jax.nn.sigmoid(field_o[every(3, 8)] * per_ocean)
         spots = [xneed[b] >> 1 for b in range(nblocks)]
         spots = [spots[b] * owned + listed(xneed[b]) for b in range(nblocks)]
 
         all_of(table.at[pl.ds(0, there * owned)], push_sem.at[1]).wait()
         for b in range(nblocks):
-            field_a[b] = dot_nt(table[spots[b]], wa[b])
-        states = [field_a[:, f, :] * per_atm for f in range(8)]
+            field_a[8 * b : 8 * b + 8] = dot_nn(table[spots[b]], turned[b])
+        states = [field_a[every(f, 8)] * per_atm for f in range(8)]
         to_atm, to_ocn = bulk_fluxes(*states, sst, uo, vo, albedo)
         for g in range(4):
             high, low = split(to_atm[g] * wet)
-            terms[:, g, :] = high
-            terms[:, g + 4, :] = high
-            terms[:, g + 8, :] = low
-            terms[:, g + 12, :] = low
+            terms[every(g, 16)] = high
+            terms[every(g + 4, 16)] = high
+            terms[every(g + 8, 16)] = low
+            terms[every(g + 12, 16)] = low
         lower = (rows >= 4).astype(jnp.int32)
         pairs = [jnp.zeros((8, blk), F32) for _ in range(npairs)]
         for b in range(nblocks):
-            cells = dot_nn(terms[b].astype(BF16), wa[b])
+            cells = dot_nn(terms[16 * b : 16 * b + 16].astype(BF16), wa[b])
             cells = cells[:8] + cells[8:]
             entry = xneed[b] - lower
             for index in range(npairs):
                 pairs[index] = pairs[index] + jnp.where(entry == 2 * index, cells, 0.0)
         for index in range(npairs):
             back_out[index] = pairs[index]
-        for index in order:
+        for index in near_first:
             for side in (0, 1):
                 remote(
                     back_out.at[index],
@@ -278,14 +286,14 @@
         remote(inverse, inverse, prep_sem.at[0], prep_sem.at[1], {"sub": 0}).start()
         for g in range(5):
             high, low = split(to_ocn[g] * wet if g < 4 else wet)
-            terms[:, g, :] = high
-            terms[:, g + 8, :] = low
+            terms[every(g, 16)] = high
+            terms[every(g + 8, 16)] = low
         for g in range(5, 8):
-            terms[:, g, :] = jnp.zeros((nblocks, blk), F32)
-            terms[:, g + 8, :] = jnp.zeros((nblocks, blk), F32)
+            terms[every(g, 16)] = jnp.zeros((nblocks, blk), F32)
+            terms[every(g + 8, 16)] = jnp.zeros((nblocks, blk), F32)
         sums = [jnp.zeros((8, blk), F32) for _ in range(2 * half)]
         for b in range(nblocks):
-            cells = dot_nn(terms[b].astype(BF16), wo[b])
+            cells = dot_nn(terms[16 * b : 16 * b + 16].astype(BF16), wo[b])
             cells = cells[:8] + cells[8:]
             entry = jnp.full((8, blk), xocn[b], jnp.int32)
             for index in range(2 * half):
@@ -301,8 +309,8 @@
         all_of(table.at[pl.ds(0, there * owned)], push_sem.at[0]).wait()
         all_of(note_out.at[pl.ds(0, there)], note_sem.at[0]).wait()
         all_of(back_in.at[pl.ds(0, there)], back_sem.at[1]).wait()
-        all_of(field_a.at[pl.ds(0, 2 * there + 1)], back_sem.at[0]).wait()
-        all_of(field_a.at[pl.ds(0, 14)], prep_sem.at[0]).wait()
+        all_of(field_a.at[pl.ds(0, 8 * (2 * there + 1))], back_sem.at[0]).wait()
+        all_of(field_a.at[pl.ds(0, 8 * 14)], prep_sem.at[0]).wait()
 
 
 def landing(back, place, inverse, ocean, atm_out, ocn_out):
@@ -349,10 +357,11 @@
             vmem((2 * nblocks, blk), F32),
             vmem((2 * nblocks, blk, blk), BF16),
             vmem((2 * nblocks, blk, blk), BF16),
-            vmem((2 * nblocks, 8, blk), F32),
-            vmem((2 * nblocks, 8, blk), F32),
-            vmem((2 * nblocks, 8, blk), F32),
-            vmem((2 * nblocks, 16, blk), F32),
+            vmem((2 * nblocks, blk, blk), BF16),
+            vmem((2 * nblocks * 8, blk), F32),
+            vmem((2 * nblocks * 8, blk), F32),
+            vmem((2 * nblocks * 8, blk), F32),
+            vmem((2 * nblocks * 16, blk), F32),
             vmem((npairs, 4, blk), F32),
             vmem((npairs, 4, blk), F32),
             vmem((npairs, 8, blk), F32),

time: 59.5 us -> 59.2 us (level)
  no operation moved by 1% of the time
where the time goes in v4:
time: 59.2 us; the launch traced here: 59.1 us
  Pallas kernels  57.8 us (98%)
  between operations  1.29 us (2%)
    pallas_call x1, Pallas kernels, per_device(): pl.pallas_call(functools.partial(kernel, ntile, npairs), out_shape=(vmem(...  57.1 us

profile of v4, /device:TPU:65, one launch (start us, length us, event | category | flops | bytes accessed | tf_op | source)
XLA Modules:
  0.0 59.1 jit_solution(2544144419524590012)
XLA Ops:
  1.3 57.1 %shard_map.113 = (f32[8,8,128]{2,1,0:T(8,128)S(1)}, f32[8,8,128]{2,1,0:T(8,128)S(1)}, f32[16,128]{1,0:T(8,128)S(1)}, f32[8,4,128]{2,1,0:T(4,128)S(1)}) custom-call(bf16[16,8,128]{2,1,0:T(8,128)(2,1)} %bitcast.14, bf16[8,4,128]{2,1,0:T(4,128)(2,1)} %bitcast.15, s32[8]{0:T(128)} %need_hbm.1, s32[8]{0:T(128)} %xneed_hbm.1, s32[8]{0:T(128)} %xocn_hbm.1, ...), custom_call_target="tpu_custom_call" | custom-call | tf_op jit(solution)/shard_map/pallas_call | solution.py:341
  58.4 0.7 %shard_map.114 = (f32[16,4,128]{2,1,0:T(4,128)}, f32[8,4,128]{2,1,0:T(4,128)}) custom-call(f32[8,8,128]{2,1,0:T(8,128)S(1)} %get-tuple-element.8.back, f32[8,8,128]{2,1,0:T(8,128)S(1)} %get-tuple-element.9.place, f32[16,128]{1,0:T(8,128)S(1)} %get-tuple-element.10.inverse, f32[8,4,128]{2,1,0:T(4,128)S(1)} %get-tuple-element.11.ocean), custom_call_target="tpu_custom_call" | custom-call | tf_op jit(solution)/shard_map/pallas_call | solution.py:392

commit v5 on v4

--- a/solution.py
+++ b/solution.py
@@ -69,7 +69,8 @@
     ocn_out,
     index_s,
     count_s,
-    table,
+    first,
+    second,
     ocean,
     sea_v,
     area_v,
@@ -96,10 +97,11 @@
     core = lax.axis_index("sub")
     nblocks, blk = wa.shape[0], wa.shape[2]
     half = nblocks // 2
-    owned = table.shape[0] // npairs
+    owned = second.shape[0] // 2
     mine = npairs // 2 - 1
     above = list(range(mine + 1, npairs - 1))
     below = list(range(mine))
+    top = above[-1]
     far_first = above[::-1] + [npairs - 1] + below
     near_first = above + [npairs - 1] + below[::-1]
     there = len(far_first)
@@ -126,21 +128,39 @@
     @pl.when(core == 0)
     def _():
         pl.semaphore_signal(barrier, inc=1, device_id={"sub": 1}, device_id_type=MESH)
+        home = pltpu.make_async_copy(atm_hbm, first.at[pl.ds(mine * owned, owned)], local_sem.at[0])
+        home.start()
         for row, source in enumerate(lists):
             pltpu.make_async_copy(source, index_s.at[0, row], local_sem.at[1]).start()
         count = pltpu.make_async_copy(count_hbm, count_s.at[0], local_sem.at[2])
         count.start()
-        pl.semaphore_wait(barrier, 1)
+        for source, target in small:
+            pltpu.make_async_copy(source, slot(target, 0), local_sem.at[3]).start()
         for source, target in large:
-            remote(source, slot(target, 0), gift_send.at[3], gift_recv.at[3], {"sub": 1}).start()
-        for source, target in small:
-            remote(source, slot(target, 0), gift_send.at[2], gift_recv.at[2], {"sub": 1}).start()
+            pltpu.make_async_copy(source, slot(target, 0), local_sem.at[4]).start()
+        home.wait()
+        pl.semaphore_wait(barrier, 2)
+        push = remote(
+            first.at[pl.ds(mine * owned, owned)],
+            second.at[pl.ds(0, owned)],
+            push_sem.at[0],
+            push_sem.at[2],
+            {"tile": asker(top), "sub": 1},
+        )
+        push.start()
+        all_of(wa, local_sem.at[4]).wait()
+        for _, target in large:
+            remote(slot(target, 0), slot(target, 0), gift_send.at[3], gift_recv.at[3], {"sub": 1}).start()
+        all_of(ocean, local_sem.at[3]).wait()
+        for _, target in small:
+            remote(slot(target, 0), slot(target, 0), gift_send.at[2], gift_recv.at[2], {"sub": 1}).start()
         all_of(index_s.at[0], local_sem.at[1]).wait()
         count.wait()
         numbers = remote(index_s.at[0], index_s.at[0], gift_send.at[0], gift_recv.at[0], {"sub": 1})
         numbers.start()
         limit = remote(count_s.at[0], count_s.at[0], gift_send.at[1], gift_recv.at[1], {"sub": 1})
         limit.start()
+        push.wait_send()
         numbers.wait_send()
         limit.wait_send()
         all_of(ocean, gift_send.at[2]).wait()
@@ -150,10 +170,11 @@
 
     @pl.when(core == 1)
     def _():
+        pl.semaphore_signal(barrier, inc=1, device_id={"tile": owner(top), "sub": 0}, device_id_type=MESH)
         for index in far_first:
             pl.semaphore_signal(barrier, inc=1, device_id={"tile": owner(index)}, device_id_type=MESH)
         pl.semaphore_signal(barrier, inc=1, device_id={"sub": 0}, device_id_type=MESH)
-        home = pltpu.make_async_copy(atm_hbm, table.at[pl.ds(mine * owned, owned)], local_sem.at[0])
+        home = pltpu.make_async_copy(atm_hbm, first.at[pl.ds(mine * owned, owned)], local_sem.at[0])
         home.start()
         for row, source in enumerate(lists):
             pltpu.make_async_copy(source, index_s.at[1, row], local_sem.at[1]).start()
@@ -165,12 +186,13 @@
             pltpu.make_async_copy(source, slot(target, 1), local_sem.at[4]).start()
         home.wait()
         pl.semaphore_wait(barrier, there + 1)
-        for index in far_first:
+        for index in far_first[1:]:
+            late = index == npairs - 1
             remote(
-                table.at[pl.ds(mine * owned, owned)],
-                table.at[pl.ds(index * owned, owned)],
+                first.at[pl.ds(mine * owned, owned)],
+                second.at[pl.ds(owned, owned)] if late else first.at[pl.ds(index * owned, owned)],
                 push_sem.at[0],
-                push_sem.at[1],
+                push_sem.at[2 if late else 1],
                 {"tile": asker(index)},
             ).start()
         all_of(index_s.at[1], local_sem.at[1]).wait()
@@ -231,56 +253,73 @@
         uo = field_o[every(1, 8)] * per_ocean
         vo = field_o[every(2, 8)] * per_ocean
         albedo = 0.06 + 0.1 * jax.nn.sigmoid(field_o[every(3, 8)] * per_ocean)
-        spots = [xneed[b] >> 1 for b in range(nblocks)]
-        spots = [spots[b] * owned + listed(xneed[b]) for b in range(nblocks)]
-
-        all_of(table.at[pl.ds(0, there * owned)], push_sem.at[1]).wait()
-        for b in range(nblocks):
-            field_a[8 * b : 8 * b + 8] = dot_nn(table[spots[b]], turned[b])
-        states = [field_a[every(f, 8)] * per_atm for f in range(8)]
-        to_atm, to_ocn = bulk_fluxes(*states, sst, uo, vo, albedo)
-        for g in range(4):
-            high, low = split(to_atm[g] * wet)
-            terms[every(g, 16)] = high
-            terms[every(g + 4, 16)] = high
-            terms[every(g + 8, 16)] = low
-            terms[every(g + 12, 16)] = low
+        homes = [xneed[b] >> 1 for b in range(nblocks)]
+        places = [listed(xneed[b]) for b in range(nblocks)]
+        early = [jnp.minimum(homes[b], top - 1) * owned + places[b] for b in range(nblocks)]
+        later = [jnp.maximum(homes[b] - top, 0) * owned + places[b] for b in range(nblocks)]
         lower = (rows >= 4).astype(jnp.int32)
-        pairs = [jnp.zeros((8, blk), F32) for _ in range(npairs)]
-        for b in range(nblocks):
-            cells = dot_nn(terms[16 * b : 16 * b + 16].astype(BF16), wa[b])
-            cells = cells[:8] + cells[8:]
-            entry = xneed[b] - lower
-            for index in range(npairs):
-                pairs[index] = pairs[index] + jnp.where(entry == 2 * index, cells, 0.0)
-        for index in range(npairs):
-            back_out[index] = pairs[index]
-        for index in near_first:
-            for side in (0, 1):
-                remote(
-                    back_out.at[index],
-                    back_in.at[index],
-                    back_sem.at[0],
-                    back_sem.at[1],
-                    {"tile": owner(index), "sub": side},
-                ).start()
-        remote(back_out.at[mine], back_in.at[mine], back_sem.at[0], back_sem.at[1], {"sub": 0}).start()
-        back_in[mine] = pairs[mine]
+
+        def fluxes():
+            states = [field_a[every(f, 8)] * per_atm for f in range(8)]
+            return bulk_fluxes(*states, sst, uo, vo, albedo)
+
+        def send_back(to_atm, indexes):
+            for g in range(4):
+                high, low = split(to_atm[g] * wet)
+                terms[every(g, 8)] = high
+                terms[every(g + 4, 8)] = low
+            pairs = {index: jnp.zeros((8, blk), F32) for index in indexes}
+            for b in range(nblocks):
+                cells = dot_nn(terms[8 * b : 8 * b + 8].astype(BF16), wa[b])
+                cells = cells + pltpu.roll(cells, 4, 0)
+                entry = xneed[b] - lower
+                for index in indexes:
+                    pairs[index] = pairs[index] + jnp.where(entry == 2 * index, cells, 0.0)
+            for index in indexes:
+                back_out[index] = pairs[index]
+            for index in indexes:
+                if index != mine:
+                    for side in (0, 1):
+                        remote(
+                            back_out.at[index],
+                            back_in.at[index],
+                            back_sem.at[0],
+                            back_sem.at[1],
+                            {"tile": owner(index), "sub": side},
+                        ).start()
+                else:
+                    remote(
+                        back_out.at[mine], back_in.at[mine], back_sem.at[0], back_sem.at[1], {"sub": 0}
+                    ).start()
+                    back_in[mine] = pairs[mine]
+
+        all_of(first.at[pl.ds(0, (there - 2) * owned)], push_sem.at[1]).wait()
+        for b in range(nblocks):
+            field_a[8 * b : 8 * b + 8] = dot_nn(first[early[b]], turned[b])
+        to_atm, _ = fluxes()
+        send_back(to_atm, [i for i in near_first if i < top] + [mine])
+        all_of(second, push_sem.at[2]).wait()
+        for b in range(nblocks):
+            far_home = jnp.full((8, blk), homes[b], jnp.int32) >= top
+            state = jnp.where(far_home, second[later[b]].astype(F32), first[early[b]].astype(F32)).astype(BF16)
+            field_a[8 * b : 8 * b + 8] = dot_nn(state, turned[b])
+        to_atm, to_ocn = fluxes()
+        send_back(to_atm, [top, npairs - 1])
 
         all_of(note_in.at[pl.ds(0, there)], note_sem.at[1]).wait()
         areas = []
-        places = []
+        spots = []
         for index in range(npairs):
             note = note_out[index] if index == mine else note_in[index]
             areas.append(note[0:2])
-            places.append(note[2:4])
+            spots.append(note[2:4])
             place[index] = jnp.concatenate(
                 [jnp.broadcast_to(note[2:3], (4, blk)), jnp.broadcast_to(note[3:4], (4, blk))], 0
             )
         areas = jnp.concatenate(areas, 0)
-        places = jnp.concatenate(places, 0)
+        spots = jnp.concatenate(spots, 0)
         for a in range(owned):
-            total = jnp.sum(jnp.where(places == float(a), areas, 0.0), 0, keepdims=True)
+            total = jnp.sum(jnp.where(spots == float(a), areas, 0.0), 0, keepdims=True)
             inverse[a : a + 1] = 1.0 / jnp.maximum(total, 1.0)
         remote(place, place, prep_sem.at[0], prep_sem.at[1], {"sub": 0}).start()
         remote(inverse, inverse, prep_sem.at[0], prep_sem.at[1], {"sub": 0}).start()
@@ -306,7 +345,7 @@
                 ocn_out[index - half] = flux
         remote(shore, ocn_out, prep_sem.at[0], prep_sem.at[1], {"sub": 0}).start()
 
-        all_of(table.at[pl.ds(0, there * owned)], push_sem.at[0]).wait()
+        all_of(first.at[pl.ds(0, (there - 1) * owned)], push_sem.at[0]).wait()
         all_of(note_out.at[pl.ds(0, there)], note_sem.at[0]).wait()
         all_of(back_in.at[pl.ds(0, there)], back_sem.at[1]).wait()
         all_of(field_a.at[pl.ds(0, 8 * (2 * there + 1))], back_sem.at[0]).wait()
@@ -351,7 +390,8 @@
         scratch_shapes=[
             pltpu.SMEM((2, 3, npairs), jnp.int32),
             pltpu.SMEM((2, 1), jnp.int32),
-            vmem((npairs * owned, fields_a, blk), BF16),
+            vmem(((npairs - 2) * owned, fields_a, blk), BF16),
+            vmem((2 * owned, fields_a, blk), BF16),
             vmem((2 * waters, fields_o, blk), BF16),
             vmem((2 * nblocks, blk), jnp.int32),
             vmem((2 * nblocks, blk), F32),
@@ -369,7 +409,7 @@
             dma((5,)),
             dma((4,)),
             dma((4,)),
-            dma((2,)),
+            dma((3,)),
             dma((2,)),
             dma((2,)),
             dma((2,)),

time: 59.2 us -> 59 us (level)
  no operation moved by 1% of the time
where the time goes in v5:
time: 59 us; the launch traced here: 58.8 us
  Pallas kernels  57.5 us (97%)
  between operations  1.29 us (2%)
    pallas_call x1, Pallas kernels, per_device(): pl.pallas_call(functools.partial(kernel, ntile, npairs), out_shape=(vmem(...  56.8 us

profile of v5, /device:TPU:65, one launch (start us, length us, event | category | flops | bytes accessed | tf_op | source)
XLA Modules:
  0.0 58.8 jit_solution(3417067877103235226)
XLA Ops:
  1.3 56.8 %shard_map.113 = (f32[8,8,128]{2,1,0:T(8,128)S(1)}, f32[8,8,128]{2,1,0:T(8,128)S(1)}, f32[16,128]{1,0:T(8,128)S(1)}, f32[8,4,128]{2,1,0:T(4,128)S(1)}) custom-call(bf16[16,8,128]{2,1,0:T(8,128)(2,1)} %bitcast.14, bf16[8,4,128]{2,1,0:T(4,128)(2,1)} %bitcast.15, s32[8]{0:T(128)} %need_hbm.1, s32[8]{0:T(128)} %xneed_hbm.1, s32[8]{0:T(128)} %xocn_hbm.1, ...), custom_call_target="tpu_custom_call" | custom-call | tf_op jit(solution)/shard_map/pallas_call | solution.py:380
  58.1 0.7 %shard_map.114 = (f32[16,4,128]{2,1,0:T(4,128)}, f32[8,4,128]{2,1,0:T(4,128)}) custom-call(f32[8,8,128]{2,1,0:T(8,128)S(1)} %get-tuple-element.8.back, f32[8,8,128]{2,1,0:T(8,128)S(1)} %get-tuple-element.9.place, f32[16,128]{1,0:T(8,128)S(1)} %get-tuple-element.10.inverse, f32[8,4,128]{2,1,0:T(4,128)S(1)} %get-tuple-element.11.ocean), custom_call_target="tpu_custom_call" | custom-call | tf_op jit(solution)/shard_map/pallas_call | solution.py:432

commit v6 on v5

--- a/solution.py
+++ b/solution.py
@@ -86,8 +86,7 @@
     back_out,
     shore,
     local_sem,
-    gift_send,
-    gift_recv,
+    gift_sem,
     push_sem,
     note_sem,
     back_sem,
@@ -97,11 +96,12 @@
     core = lax.axis_index("sub")
     nblocks, blk = wa.shape[0], wa.shape[2]
     half = nblocks // 2
-    owned = second.shape[0] // 2
+    owned = second.shape[0] // 3
     mine = npairs // 2 - 1
     above = list(range(mine + 1, npairs - 1))
     below = list(range(mine))
     top = above[-1]
+    cut = top - 1
     far_first = above[::-1] + [npairs - 1] + below
     near_first = above + [npairs - 1] + below[::-1]
     there = len(far_first)
@@ -142,7 +142,7 @@
         pl.semaphore_wait(barrier, 2)
         push = remote(
             first.at[pl.ds(mine * owned, owned)],
-            second.at[pl.ds(0, owned)],
+            second.at[pl.ds(owned, owned)],
             push_sem.at[0],
             push_sem.at[2],
             {"tile": asker(top), "sub": 1},
@@ -150,28 +150,28 @@
         push.start()
         all_of(wa, local_sem.at[4]).wait()
         for _, target in large:
-            remote(slot(target, 0), slot(target, 0), gift_send.at[3], gift_recv.at[3], {"sub": 1}).start()
+            remote(slot(target, 0), slot(target, 0), gift_sem.at[3], gift_sem.at[3], {"sub": 1}).start()
         all_of(ocean, local_sem.at[3]).wait()
         for _, target in small:
-            remote(slot(target, 0), slot(target, 0), gift_send.at[2], gift_recv.at[2], {"sub": 1}).start()
+            remote(slot(target, 0), slot(target, 0), gift_sem.at[2], gift_sem.at[2], {"sub": 1}).start()
         all_of(index_s.at[0], local_sem.at[1]).wait()
         count.wait()
-        numbers = remote(index_s.at[0], index_s.at[0], gift_send.at[0], gift_recv.at[0], {"sub": 1})
+        numbers = remote(index_s.at[0], index_s.at[0], gift_sem.at[0], gift_sem.at[0], {"sub": 1})
         numbers.start()
-        limit = remote(count_s.at[0], count_s.at[0], gift_send.at[1], gift_recv.at[1], {"sub": 1})
+        limit = remote(count_s.at[0], count_s.at[0], gift_sem.at[1], gift_sem.at[1], {"sub": 1})
         limit.start()
         push.wait_send()
         numbers.wait_send()
         limit.wait_send()
-        all_of(ocean, gift_send.at[2]).wait()
-        all_of(wa, gift_send.at[3]).wait()
-        all_of(field_a.at[pl.ds(0, 8 * 14)], prep_sem.at[1]).wait()
+        all_of(ocean, gift_sem.at[2]).wait()
+        all_of(wa, gift_sem.at[3]).wait()
+        all_of(field_a.at[pl.ds(0, 8 * 14)], prep_sem).wait()
         all_of(back_in, back_sem.at[1]).wait()
 
     @pl.when(core == 1)
     def _():
         pl.semaphore_signal(barrier, inc=1, device_id={"tile": owner(top), "sub": 0}, device_id_type=MESH)
-        for index in far_first:
+        for index in near_first:
             pl.semaphore_signal(barrier, inc=1, device_id={"tile": owner(index)}, device_id_type=MESH)
         pl.semaphore_signal(barrier, inc=1, device_id={"sub": 0}, device_id_type=MESH)
         home = pltpu.make_async_copy(atm_hbm, first.at[pl.ds(mine * owned, owned)], local_sem.at[0])
@@ -187,10 +187,10 @@
         home.wait()
         pl.semaphore_wait(barrier, there + 1)
         for index in far_first[1:]:
-            late = index == npairs - 1
+            late = index >= cut
             remote(
                 first.at[pl.ds(mine * owned, owned)],
-                second.at[pl.ds(owned, owned)] if late else first.at[pl.ds(index * owned, owned)],
+                second.at[pl.ds((index - cut) * owned, owned)] if late else first.at[pl.ds(index * owned, owned)],
                 push_sem.at[0],
                 push_sem.at[2 if late else 1],
                 {"tile": asker(index)},
@@ -199,10 +199,10 @@
         count.wait()
         all_of(ocean, local_sem.at[3]).wait()
         all_of(wa, local_sem.at[4]).wait()
-        all_of(index_s.at[0], gift_recv.at[0]).wait()
-        all_of(count_s.at[0], gift_recv.at[1]).wait()
-        all_of(ocean, gift_recv.at[2]).wait()
-        all_of(wa, gift_recv.at[3]).wait()
+        all_of(index_s.at[0], gift_sem.at[0]).wait()
+        all_of(count_s.at[0], gift_sem.at[1]).wait()
+        all_of(ocean, gift_sem.at[2]).wait()
+        all_of(wa, gift_sem.at[3]).wait()
 
         def every(first, stride):
             return pl.ds(first, nblocks, stride=stride), slice(None)
@@ -255,8 +255,8 @@
         albedo = 0.06 + 0.1 * jax.nn.sigmoid(field_o[every(3, 8)] * per_ocean)
         homes = [xneed[b] >> 1 for b in range(nblocks)]
         places = [listed(xneed[b]) for b in range(nblocks)]
-        early = [jnp.minimum(homes[b], top - 1) * owned + places[b] for b in range(nblocks)]
-        later = [jnp.maximum(homes[b] - top, 0) * owned + places[b] for b in range(nblocks)]
+        early = [jnp.minimum(homes[b], cut - 1) * owned + places[b] for b in range(nblocks)]
+        later = [jnp.maximum(homes[b] - cut, 0) * owned + places[b] for b in range(nblocks)]
         lower = (rows >= 4).astype(jnp.int32)
 
         def fluxes():
@@ -293,18 +293,18 @@
                     ).start()
                     back_in[mine] = pairs[mine]
 
-        all_of(first.at[pl.ds(0, (there - 2) * owned)], push_sem.at[1]).wait()
+        all_of(first.at[pl.ds(0, (there - 3) * owned)], push_sem.at[1]).wait()
         for b in range(nblocks):
             field_a[8 * b : 8 * b + 8] = dot_nn(first[early[b]], turned[b])
         to_atm, _ = fluxes()
-        send_back(to_atm, [i for i in near_first if i < top] + [mine])
+        send_back(to_atm, [i for i in near_first if i < cut] + [mine])
         all_of(second, push_sem.at[2]).wait()
         for b in range(nblocks):
-            far_home = jnp.full((8, blk), homes[b], jnp.int32) >= top
+            far_home = jnp.full((8, blk), homes[b], jnp.int32) >= cut
             state = jnp.where(far_home, second[later[b]].astype(F32), first[early[b]].astype(F32)).astype(BF16)
             field_a[8 * b : 8 * b + 8] = dot_nn(state, turned[b])
         to_atm, to_ocn = fluxes()
-        send_back(to_atm, [top, npairs - 1])
+        send_back(to_atm, [cut, top, npairs - 1])
 
         all_of(note_in.at[pl.ds(0, there)], note_sem.at[1]).wait()
         areas = []
@@ -321,8 +321,8 @@
         for a in range(owned):
             total = jnp.sum(jnp.where(spots == float(a), areas, 0.0), 0, keepdims=True)
             inverse[a : a + 1] = 1.0 / jnp.maximum(total, 1.0)
-        remote(place, place, prep_sem.at[0], prep_sem.at[1], {"sub": 0}).start()
-        remote(inverse, inverse, prep_sem.at[0], prep_sem.at[1], {"sub": 0}).start()
+        remote(place, place, prep_sem, prep_sem, {"sub": 0}).start()
+        remote(inverse, inverse, prep_sem, prep_sem, {"sub": 0}).start()
         for g in range(5):
             high, low = split(to_ocn[g] * wet if g < 4 else wet)
             terms[every(g, 16)] = high
@@ -343,13 +343,13 @@
                 shore[index] = flux
             else:
                 ocn_out[index - half] = flux
-        remote(shore, ocn_out, prep_sem.at[0], prep_sem.at[1], {"sub": 0}).start()
-
-        all_of(first.at[pl.ds(0, (there - 1) * owned)], push_sem.at[0]).wait()
+        remote(shore, ocn_out, prep_sem, prep_sem, {"sub": 0}).start()
+
+        all_of(wa.at[pl.ds(0, there - 1)], push_sem.at[0]).wait()
         all_of(note_out.at[pl.ds(0, there)], note_sem.at[0]).wait()
         all_of(back_in.at[pl.ds(0, there)], back_sem.at[1]).wait()
         all_of(field_a.at[pl.ds(0, 8 * (2 * there + 1))], back_sem.at[0]).wait()
-        all_of(field_a.at[pl.ds(0, 8 * 14)], prep_sem.at[0]).wait()
+        all_of(field_a.at[pl.ds(0, 8 * 14)], prep_sem).wait()
 
 
 def landing(back, place, inverse, ocean, atm_out, ocn_out):
@@ -390,8 +390,8 @@
         scratch_shapes=[
             pltpu.SMEM((2, 3, npairs), jnp.int32),
             pltpu.SMEM((2, 1), jnp.int32),
-            vmem(((npairs - 2) * owned, fields_a, blk), BF16),
-            vmem((2 * owned, fields_a, blk), BF16),
+            vmem(((npairs - 3) * owned, fields_a, blk), BF16),
+            vmem((3 * owned, fields_a, blk), BF16),
             vmem((2 * waters, fields_o, blk), BF16),
             vmem((2 * nblocks, blk), jnp.int32),
             vmem((2 * nblocks, blk), F32),
@@ -408,11 +408,10 @@
             vmem((waters, nflux, blk), F32),
             dma((5,)),
             dma((4,)),
-            dma((4,)),
             dma((3,)),
             dma((2,)),
             dma((2,)),
-            dma((2,)),
+            dma,
         ],
         compiler_params=pltpu.CompilerParams(
             collective_id=0, has_side_effects=True, vmem_limit_bytes=VMEM_LIMIT

time: 59 us -> 58.9 us (level)
  no operation moved by 1% of the time
where the time goes in v6:
time: 58.9 us; the launch traced here: 58.8 us
  Pallas kernels  57.5 us (98%)
  between operations  1.29 us (2%)
    pallas_call x1, Pallas kernels, per_device(): pl.pallas_call(functools.partial(kernel, ntile, npairs), out_shape=(vmem(...  56.8 us

profile of v6, /device:TPU:65, one launch (start us, length us, event | category | flops | bytes accessed | tf_op | source)
XLA Modules:
  0.0 58.8 jit_solution(9392689766269102084)
XLA Ops:
  1.3 56.8 %shard_map.113 = (f32[8,8,128]{2,1,0:T(8,128)S(1)}, f32[8,8,128]{2,1,0:T(8,128)S(1)}, f32[16,128]{1,0:T(8,128)S(1)}, f32[8,4,128]{2,1,0:T(4,128)S(1)}) custom-call(bf16[16,8,128]{2,1,0:T(8,128)(2,1)} %bitcast.14, bf16[8,4,128]{2,1,0:T(4,128)(2,1)} %bitcast.15, s32[8]{0:T(128)} %need_hbm.1, s32[8]{0:T(128)} %xneed_hbm.1, s32[8]{0:T(128)} %xocn_hbm.1, ...), custom_call_target="tpu_custom_call" | custom-call | tf_op jit(solution)/shard_map/pallas_call | solution.py:380
  58.1 0.7 %shard_map.114 = (f32[16,4,128]{2,1,0:T(4,128)}, f32[8,4,128]{2,1,0:T(4,128)}) custom-call(f32[8,8,128]{2,1,0:T(8,128)S(1)} %get-tuple-element.8.back, f32[8,8,128]{2,1,0:T(8,128)S(1)} %get-tuple-element.9.place, f32[16,128]{1,0:T(8,128)S(1)} %get-tuple-element.10.inverse, f32[8,4,128]{2,1,0:T(4,128)S(1)} %get-tuple-element.11.ocean), custom_call_target="tpu_custom_call" | custom-call | tf_op jit(solution)/shard_map/pallas_call | solution.py:431

commit v7 on v6

--- a/solution.py
+++ b/solution.py
@@ -139,15 +139,15 @@
         for source, target in large:
             pltpu.make_async_copy(source, slot(target, 0), local_sem.at[4]).start()
         home.wait()
-        pl.semaphore_wait(barrier, 2)
-        push = remote(
-            first.at[pl.ds(mine * owned, owned)],
-            second.at[pl.ds(owned, owned)],
-            push_sem.at[0],
-            push_sem.at[2],
-            {"tile": asker(top), "sub": 1},
-        )
-        push.start()
+        pl.semaphore_wait(barrier, 3)
+        for index in (top, npairs - 1):
+            remote(
+                first.at[pl.ds(mine * owned, owned)],
+                second.at[pl.ds((index - cut) * owned, owned)],
+                push_sem.at[0],
+                push_sem.at[2],
+                {"tile": asker(index), "sub": 1},
+            ).start()
         all_of(wa, local_sem.at[4]).wait()
         for _, target in large:
             remote(slot(target, 0), slot(target, 0), gift_sem.at[3], gift_sem.at[3], {"sub": 1}).start()
@@ -160,7 +160,7 @@
         numbers.start()
         limit = remote(count_s.at[0], count_s.at[0], gift_sem.at[1], gift_sem.at[1], {"sub": 1})
         limit.start()
-        push.wait_send()
+        all_of(first.at[pl.ds(0, 2 * owned)], push_sem.at[0]).wait()
         numbers.wait_send()
         limit.wait_send()
         all_of(ocean, gift_sem.at[2]).wait()
@@ -172,7 +172,10 @@
     def _():
         pl.semaphore_signal(barrier, inc=1, device_id={"tile": owner(top), "sub": 0}, device_id_type=MESH)
         for index in near_first:
-            pl.semaphore_signal(barrier, inc=1, device_id={"tile": owner(index)}, device_id_type=MESH)
+            side = 0 if index == npairs - 1 else 1
+            pl.semaphore_signal(
+                barrier, inc=1, device_id={"tile": owner(index), "sub": side}, device_id_type=MESH
+            )
         pl.semaphore_signal(barrier, inc=1, device_id={"sub": 0}, device_id_type=MESH)
         home = pltpu.make_async_copy(atm_hbm, first.at[pl.ds(mine * owned, owned)], local_sem.at[0])
         home.start()
@@ -185,8 +188,8 @@
         for source, target in large:
             pltpu.make_async_copy(source, slot(target, 1), local_sem.at[4]).start()
         home.wait()
-        pl.semaphore_wait(barrier, there + 1)
-        for index in far_first[1:]:
+        pl.semaphore_wait(barrier, there)
+        for index in [i for i in far_first[1:] if i != npairs - 1]:
             late = index >= cut
             remote(
                 first.at[pl.ds(mine * owned, owned)],
@@ -235,10 +238,15 @@
             note_out[index, 0:2] = held[at : at + 2]
             for k in range(2):
                 note_out[index, 2 + k : 3 + k] = jnp.full((1, blk), listed(2 * index + k), jnp.int32).astype(F32)
-        for index in far_first:
+
+        def send_note(index):
             remote(
                 note_out.at[index], note_in.at[index], note_sem.at[0], note_sem.at[1], {"tile": owner(index)}
             ).start()
+
+        for index in far_first:
+            if index != npairs - 1:
+                send_note(index)
 
         for b in range(nblocks):
             state = ocean[xocn[b]].astype(F32)
@@ -299,6 +307,7 @@
         to_atm, _ = fluxes()
         send_back(to_atm, [i for i in near_first if i < cut] + [mine])
         all_of(second, push_sem.at[2]).wait()
+        send_note(npairs - 1)
         for b in range(nblocks):
             far_home = jnp.full((8, blk), homes[b], jnp.int32) >= cut
             state = jnp.where(far_home, second[later[b]].astype(F32), first[early[b]].astype(F32)).astype(BF16)
@@ -345,7 +354,7 @@
                 ocn_out[index - half] = flux
         remote(shore, ocn_out, prep_sem, prep_sem, {"sub": 0}).start()
 
-        all_of(wa.at[pl.ds(0, there - 1)], push_sem.at[0]).wait()
+        all_of(wa.at[pl.ds(0, there - 2)], push_sem.at[0]).wait()
         all_of(note_out.at[pl.ds(0, there)], note_sem.at[0]).wait()
         all_of(back_in.at[pl.ds(0, there)], back_sem.at[1]).wait()
         all_of(field_a.at[pl.ds(0, 8 * (2 * there + 1))], back_sem.at[0]).wait()

time: 58.9 us -> 58.4 us (level)
  Pallas kernels: 57.5 us -> 56.9 us
where the time goes in v7:
time: 58.4 us; the launch traced here: 58.2 us
  Pallas kernels  56.9 us (97%)
  between operations  1.29 us (2%)
    pallas_call x1, Pallas kernels, per_device(): pl.pallas_call(functools.partial(kernel, ntile, npairs), out_shape=(vmem(...  56.2 us

profile of v7, /device:TPU:65, one launch (start us, length us, event | category | flops | bytes accessed | tf_op | source)
XLA Modules:
  0.0 58.2 jit_solution(6620911250880187721)
XLA Ops:
  1.3 56.2 %shard_map.113 = (f32[8,8,128]{2,1,0:T(8,128)S(1)}, f32[8,8,128]{2,1,0:T(8,128)S(1)}, f32[16,128]{1,0:T(8,128)S(1)}, f32[8,4,128]{2,1,0:T(4,128)S(1)}) custom-call(bf16[16,8,128]{2,1,0:T(8,128)(2,1)} %bitcast.14, bf16[8,4,128]{2,1,0:T(4,128)(2,1)} %bitcast.15, s32[8]{0:T(128)} %need_hbm.1, s32[8]{0:T(128)} %xneed_hbm.1, s32[8]{0:T(128)} %xocn_hbm.1, ...), custom_call_target="tpu_custom_call" | custom-call | tf_op jit(solution)/shard_map/pallas_call | solution.py:389
  57.5 0.7 %shard_map.114 = (f32[16,4,128]{2,1,0:T(4,128)}, f32[8,4,128]{2,1,0:T(4,128)}) custom-call(f32[8,8,128]{2,1,0:T(8,128)S(1)} %get-tuple-element.8.back, f32[8,8,128]{2,1,0:T(8,128)S(1)} %get-tuple-element.9.place, f32[16,128]{1,0:T(8,128)S(1)} %get-tuple-element.10.inverse, f32[8,4,128]{2,1,0:T(4,128)S(1)} %get-tuple-element.11.ocean), custom_call_target="tpu_custom_call" | custom-call | tf_op jit(solution)/shard_map/pallas_call | solution.py:440

commit v8 on v7

--- a/solution.py
+++ b/solution.py
@@ -202,6 +202,13 @@
         count.wait()
         all_of(ocean, local_sem.at[3]).wait()
         all_of(wa, local_sem.at[4]).wait()
+
+        def turn(blocks):
+            for b in blocks:
+                turned[b] = wa[b].T
+                sums_a[8 * b : 8 * b + 8] = dot_nn(jnp.ones((8, blk), BF16), turned[b])
+
+        turn(range(half, nblocks))
         all_of(index_s.at[0], gift_sem.at[0]).wait()
         all_of(count_s.at[0], gift_sem.at[1]).wait()
         all_of(ocean, gift_sem.at[2]).wait()
@@ -252,9 +259,7 @@
             state = ocean[xocn[b]].astype(F32)
             left = jnp.concatenate([state, jnp.ones((8 - state.shape[0], blk), F32)], 0).astype(BF16)
             field_o[8 * b : 8 * b + 8] = dot_nt(left, wo[b])
-        for b in range(nblocks):
-            turned[b] = wa[b].T
-            sums_a[8 * b : 8 * b + 8] = dot_nn(jnp.ones((8, blk), BF16), turned[b])
+        turn(range(half))
         per_ocean = 1.0 / field_o[every(4, 8)]
         per_atm = 1.0 / sums_a[every(0, 8)]
         sst = field_o[every(0, 8)] * per_ocean

time: 58.4 us -> 58.4 us (level)
  no operation moved by 1% of the time
where the time goes in v8:
time: 58.4 us; the launch traced here: 58.2 us
  Pallas kernels  56.9 us (97%)
  between operations  1.29 us (2%)
    pallas_call x1, Pallas kernels, per_device(): pl.pallas_call(functools.partial(kernel, ntile, npairs), out_shape=(vmem(...  56.2 us

profile of v8, /device:TPU:65, one launch (start us, length us, event | category | flops | bytes accessed | tf_op | source)
XLA Modules:
  0.0 58.2 jit_solution(176701082914253789)
XLA Ops:
  1.3 56.2 %shard_map.113 = (f32[8,8,128]{2,1,0:T(8,128)S(1)}, f32[8,8,128]{2,1,0:T(8,128)S(1)}, f32[16,128]{1,0:T(8,128)S(1)}, f32[8,4,128]{2,1,0:T(4,128)S(1)}) custom-call(bf16[16,8,128]{2,1,0:T(8,128)(2,1)} %bitcast.14, bf16[8,4,128]{2,1,0:T(4,128)(2,1)} %bitcast.15, s32[8]{0:T(128)} %need_hbm.1, s32[8]{0:T(128)} %xneed_hbm.1, s32[8]{0:T(128)} %xocn_hbm.1, ...), custom_call_target="tpu_custom_call" | custom-call | tf_op jit(solution)/shard_map/pallas_call | solution.py:394
  57.5 0.7 %shard_map.114 = (f32[16,4,128]{2,1,0:T(4,128)}, f32[8,4,128]{2,1,0:T(4,128)}) custom-call(f32[8,8,128]{2,1,0:T(8,128)S(1)} %get-tuple-element.8.back, f32[8,8,128]{2,1,0:T(8,128)S(1)} %get-tuple-element.9.place, f32[16,128]{1,0:T(8,128)S(1)} %get-tuple-element.10.inverse, f32[8,4,128]{2,1,0:T(4,128)S(1)} %get-tuple-element.11.ocean), custom_call_target="tpu_custom_call" | custom-call | tf_op jit(solution)/shard_map/pallas_call | solution.py:445

commit v9 on v7

--- a/solution.py
+++ b/solution.py
@@ -171,7 +171,7 @@
     @pl.when(core == 1)
     def _():
         pl.semaphore_signal(barrier, inc=1, device_id={"tile": owner(top), "sub": 0}, device_id_type=MESH)
-        for index in near_first:
+        for index in [npairs - 1] + [i for i in near_first if i != npairs - 1]:
             side = 0 if index == npairs - 1 else 1
             pl.semaphore_signal(
                 barrier, inc=1, device_id={"tile": owner(index), "sub": side}, device_id_type=MESH

time: 58.4 us -> 58.4 us (level)
  no operation moved by 1% of the time
where the time goes in v9:
time: 58.4 us; the launch traced here: 58.2 us
  Pallas kernels  56.9 us (97%)
  between operations  1.29 us (2%)
    pallas_call x1, Pallas kernels, per_device(): pl.pallas_call(functools.partial(kernel, ntile, npairs), out_shape=(vmem(...  56.2 us

profile of v9, /device:TPU:65, one launch (start us, length us, event | category | flops | bytes accessed | tf_op | source)
XLA Modules:
  0.0 58.2 jit_solution(6904553765864490432)
XLA Ops:
  1.3 56.2 %shard_map.113 = (f32[8,8,128]{2,1,0:T(8,128)S(1)}, f32[8,8,128]{2,1,0:T(8,128)S(1)}, f32[16,128]{1,0:T(8,128)S(1)}, f32[8,4,128]{2,1,0:T(4,128)S(1)}) custom-call(bf16[16,8,128]{2,1,0:T(8,128)(2,1)} %bitcast.14, bf16[8,4,128]{2,1,0:T(4,128)(2,1)} %bitcast.15, s32[8]{0:T(128)} %need_hbm.1, s32[8]{0:T(128)} %xneed_hbm.1, s32[8]{0:T(128)} %xocn_hbm.1, ...), custom_call_target="tpu_custom_call" | custom-call | tf_op jit(solution)/shard_map/pallas_call | solution.py:389
  57.5 0.7 %shard_map.114 = (f32[16,4,128]{2,1,0:T(4,128)}, f32[8,4,128]{2,1,0:T(4,128)}) custom-call(f32[8,8,128]{2,1,0:T(8,128)S(1)} %get-tuple-element.8.back, f32[8,8,128]{2,1,0:T(8,128)S(1)} %get-tuple-element.9.place, f32[16,128]{1,0:T(8,128)S(1)} %get-tuple-element.10.inverse, f32[8,4,128]{2,1,0:T(4,128)S(1)} %get-tuple-element.11.ocean), custom_call_target="tpu_custom_call" | custom-call | tf_op jit(solution)/shard_map/pallas_call | solution.py:440
